TPU v7x, 128 devices: a whole 4x4x4 slice. The times are simulated.
128 devices in a mesh: region: 16 (over y_lo, z, core), depth: 2 (over y_hi), member: 4 (over x).
Axes of the slice: x: 4, y: 4 (y_hi: 2, y_lo: 2; y = y_hi * 2 + y_lo), z: 4, core: 2. Of those that a mesh axis runs over, the one named last changes fastest.
Arguments:
- ensemble: bfloat16 [14, 384, 16384], P('depth', 'member', 'region'), may hold values from -6 to 6
- obs_weights: float32 [14], P('depth'), may hold values from -1.5 to 1.5
- obs_tiles: int32 [8192], P('region'), may hold values from 0 to 1023
- obs_values: float32 [8192], P('region'), may hold values from -8 to 8
- obs_error: float32 [8192], P('region'), may hold values from 0.2 to 2
- obs_noise: float32 [384, 8192], P('member', 'region'), may hold values from -6 to 6
Outputs:
- analysis: bfloat16 [14, 384, 16384], P('depth', 'member', 'region')
- inflation: float32 [], replicated
Inputs may be any that keep to these rules, and one draw needn't show every extreme that they name: `obs_tiles`: the tile of the observation, counted within the 1024 tiles of the region whose block holds the observation.
All inputs are finite; a program needn't handle non-finite values.
Results may differ from a plain program's by a relative error of at most 0.011.
Values may be sent and summed in bfloat16 or wider, within the bound.
A program may use at most 64 MiB of HBM per device.

v0:
```python
import jax
import jax.numpy as jnp
from jax import lax
from jax.sharding import PartitionSpec as P

MEMBERS = 384
RADIUS = 1024


def sent_to_all(array, axis):
    copies = jnp.broadcast_to(array, (lax.axis_size(axis), *array.shape))
    return lax.all_to_all(copies, axis, split_axis=0, concat_axis=0, tiled=True)


def taken_together(array, axis):
    return sent_to_all(array, axis).astype(jnp.float32).sum(axis=0)


def over_copies(array, axis):
    return sent_to_all(array, axis).sum(axis=0)


def in_one(arrays, axis):
    flat, at, done = (jnp.concatenate([a.reshape(-1) for a in arrays]), 0, [])
    total = over_copies(flat, axis)
    for a in arrays:
        done.append(total[at : at + a.size].reshape(a.shape))
        at += a.size
    return tuple(done)


def extended(array, sides, width):
    for axis, dim in sides:
        peers, length = (lax.axis_size(axis), array.shape[dim])
        up = [(i, (i + 1) % peers) for i in range(peers - 1)]
        down = [(j, i) for i, j in up]
        last = lax.slice_in_dim(array, length - width, length, axis=dim)
        leading = lax.slice_in_dim(array, 0, width, axis=dim)
        before = lax.ppermute(last, axis, up)
        after = lax.ppermute(leading, axis, down)
        array = jnp.concatenate([before, array, after], axis=dim)
    return array


def sent_together(arrays, axis, dim, along):
    both = jnp.concatenate(arrays, axis=along)
    out, at, done = (lax.all_gather(both, axis, axis=dim, tiled=True), 0, [])
    for a in arrays:
        done.append(lax.slice_in_dim(out, at, at + a.shape[along], axis=along))
        at += a.shape[along]
    return tuple(done)


def in_blocks(array, dim, peers):
    before, after = (array.shape[:dim], array.shape[dim + 1 :])
    return jnp.moveaxis(array.reshape(*before, peers, -1, *after), dim, 0)


def cut_rows(length, count):
    unit = 8 if length >= 8 * count else 1
    return [length // unit * k // count * unit for k in range(1, count)]


def laid_out(parts, dim):
    parts = jnp.moveaxis(parts, 0, dim)
    dims = parts.shape
    return parts.reshape(*dims[:dim], dims[dim] * dims[dim + 1], *dims[dim + 2 :])


def exchange_in_pieces(array, axis, pieces, split_dim, concat_dim):
    parts = in_blocks(array, split_dim, lax.axis_size(axis))
    widest = max(range(1, max(2, parts.ndim - 1)), key=lambda d: parts.shape[d])
    done = []
    for section in jnp.split(parts, cut_rows(parts.shape[widest], pieces), axis=widest):
        if section.size:
            done.append(lax.all_to_all(section, axis, split_axis=0, concat_axis=0, tiled=True))
    return laid_out(jnp.concatenate(done, axis=widest), concat_dim)


def regress(
    anomalies, own_anom, state_mean, obs_anom, perturbed, factor, obs_pos, first_tile, infl_root
):
    var_count = anomalies.shape[0]
    tile_count = anomalies.shape[2]
    block = 128

    def one_block(block_index, output):
        block_start = block_index * block
        slab = lax.dynamic_slice_in_dim(anomalies, block_start, block, 2)
        own_slab = lax.dynamic_slice_in_dim(own_anom, block_start, block, 2)
        means = lax.dynamic_slice_in_dim(state_mean, block_start, block, 1)
        covariance = jnp.einsum(
            "lmt,mj->ltj", slab, obs_anom, preferred_element_type=jnp.float32
        ) / (MEMBERS - 1)
        tile_pos = (first_tile + block_start + jnp.arange(block, dtype=jnp.int32)).astype(
            jnp.float32
        )
        closeness = jnp.maximum(0.0, 1.0 - jnp.abs(tile_pos[:, None] - obs_pos[None, :]) / RADIUS)
        kalman_gain = (covariance * (closeness * closeness * factor[None, :])[None]).astype(
            jnp.bfloat16
        )
        increment = jnp.einsum(
            "ltj,mj->lmt", kalman_gain, perturbed, preferred_element_type=jnp.float32
        )
        updated = (means[:, None, :] + infl_root * own_slab.astype(jnp.float32) + increment).astype(
            jnp.bfloat16
        )
        return lax.dynamic_update_slice_in_dim(output, updated, block_start, 2)

    output = jnp.zeros((var_count, perturbed.shape[0], tile_count), jnp.bfloat16)
    return lax.fori_loop(0, tile_count // block, one_block, output)


def shards(ensemble, obs_weights, obs_tiles, obs_values, obs_error, obs_noise):
    tile_count = ensemble.shape[2]
    own_members = ensemble.shape[1]
    obs_count = obs_tiles.shape[0]
    member_sum = jnp.sum(ensemble, axis=1, dtype=jnp.float32)
    picked = jnp.take(ensemble, obs_tiles, axis=2).astype(jnp.float32)
    partial_pred = jnp.einsum("lmk,l->mk", picked, obs_weights, precision=lax.Precision.HIGHEST)
    predicted = taken_together(partial_pred.astype(jnp.bfloat16), "depth").astype(jnp.float32)
    totals = in_one(
        (member_sum, jnp.sum(predicted, axis=0), jnp.sum(predicted * predicted, axis=0)), "member"
    )
    state_mean = totals[0] / MEMBERS
    obs_mean = totals[1] / MEMBERS
    obs_dev = predicted - obs_mean[None, :]
    obs_spread = (totals[2] - MEMBERS * obs_mean * obs_mean) / (MEMBERS - 1)
    innovation = obs_values - obs_mean
    global_sums = in_one(
        (jnp.sum(innovation * innovation), jnp.sum(obs_spread + obs_error)), "region"
    )
    inflation = global_sums[0] / global_sums[1]
    infl_root = jnp.sqrt(inflation)
    factor = inflation / (inflation * obs_spread + obs_error)
    obs_anom = obs_dev.astype(jnp.bfloat16)
    perturbed = (
        innovation[None, :] + jnp.sqrt(obs_error)[None, :] * obs_noise - infl_root * obs_dev
    ).astype(jnp.bfloat16)
    first_tile = lax.axis_index("region") * tile_count
    obs_pos = (first_tile + obs_tiles).astype(jnp.float32)
    stacked = jnp.concatenate([obs_anom, perturbed], axis=0)
    widened = extended(stacked, (("region", 1),), obs_count)
    near_anom = widened[:own_members]
    near_pert = widened[own_members:]
    scalars = jnp.stack([factor, obs_pos], axis=0)
    wide_scalars = extended(scalars, (("region", 1),), obs_count)
    near_factor = wide_scalars[0]
    near_pos = wide_scalars[1]
    anomalies = (ensemble.astype(jnp.float32) - state_mean[:, None, :]).astype(jnp.bfloat16)
    all_obs_anom, all_pert = sent_together((near_anom, near_pert), "member", 0, 1)
    share = tile_count // lax.axis_size("member")
    offset = lax.axis_index("member") * share
    split_anom = exchange_in_pieces(anomalies, "member", 2, 2, 1)
    split_mean = lax.dynamic_slice_in_dim(state_mean, offset, share, 1)
    updated = regress(
        split_anom,
        split_anom,
        split_mean,
        all_obs_anom,
        all_pert,
        near_factor,
        near_pos,
        first_tile + offset,
        infl_root,
    )
    analysis = lax.all_to_all(updated, "member", split_axis=1, concat_axis=2, tiled=True)
    return (analysis, inflation)


def solution(mesh):
    return jax.shard_map(
        shards,
        mesh=mesh,
        in_specs=(
            P("depth", "member", "region"),
            P("depth"),
            P("region"),
            P("region"),
            P("region"),
            P("member", "region"),
        ),
        out_specs=(P("depth", "member", "region"), P()),
        check_vma=False,
    )
```

profile of v0, /device:TPU:1, one launch (start us, length us, event | category | flops | bytes accessed | tf_op | source)
XLA Modules:
  0.0 160.2 jit_solution(6960265160344156900)
XLA Ops:
  8.6 3.2 %copy.36 = bf16[7,96,1024]{1,0,2:T(8,128)(2,1)S(1)} copy(bf16[7,96,1024]{2,1,0:T(8,128)(2,1)} %param.8) | data formatting | bytes 2752512 | tf_op args[0]
  11.8 1.8 %gather_fusion = bf16[512,7,96]{2,1,0:T(8,128)(2,1)S(1)} fusion(bf16[7,96,1024]{1,0,2:T(8,128)(2,1)S(1)} %copy.36, s32[1024]{0:T(1024)S(1)} %pad_clamp_fusion), kind=kCustom, calls=%fused_computation | custom fusion | bytes 1378304 | tf_op jit(solution)/shard_map/jit(_take)/gather | solution.py:119
  13.6 1.8 %select_bitcast_fusion = bf16[7,96,512]{1,0,2:T(8,128)(2,1)S(1)} fusion(bf16[512,7,96]{2,1,0:T(8,128)(2,1)S(1)} %gather_fusion, pred[512]{0:T(512)(128)(4,1)S(1)} %compare_and_fusion), kind=kLoop, calls=%fused_computation.15 | loop fusion | flops 344064 | bytes 1376768 | tf_op jit(solution)/shard_map/jit(_take)/select_n | solution.py:119
  17.9 5.0 %all-to-all-start = ((bf16[2,96,512]{2,1,0:T(8,128)(2,1)}), bf16[2,96,512]{2,1,0:T(8,128)(2,1)S(1)}, u32[]{:S(2)}, u32[]{:S(2)}) async-start(bf16[2,96,512]{2,1,0:T(8,128)(2,1)} %broadcast_in_dim.41), calls=%async_computation | async-start | bytes 393216 | tf_op jit(solution)/shard_map/all_to_all | solution.py:12
  23.3 4.8 %all-to-all-done = bf16[2,96,512]{2,1,0:T(8,128)(2,1)S(1)} async-done(((bf16[2,96,512]{2,1,0:T(8,128)(2,1)}), bf16[2,96,512]{2,1,0:T(8,128)(2,1)S(1)}, u32[]{:S(2)}, u32[]{:S(2)}) %all-to-all-start) | async-done | bytes 196640 | tf_op jit(solution)/shard_map/all_to_all | solution.py:12
  28.3 8.6 %all_to_all.45 = f32[4,1,8192]{2,1,0:T(1,128)S(1)} all-to-all(f32[4,1,8192]{2,1,0:T(1,128)S(1)} %broadcast_in_dim.42), channel_id=1, replica_groups=mesh['region'=16,'depth'=2,'member'=4] {'member'}, dimensions={0} | all-to-all | bytes 262144 | tf_op jit(solution)/shard_map/all_to_all | solution.py:12
  37.7 1.4 pad_maximum_fusion.7
  39.1 14.3 %all_to_all.46 = f32[16,1,2]{2,1,0:T(1,128)S(1)} all-to-all(f32[16,1,2]{2,1,0:T(1,128)S(1)} %broadcast_in_dim.43), channel_id=1, replica_groups=mesh['region'=16,'depth'=2,'member'=4] {'region'}, dimensions={0} | all-to-all | bytes 256 | tf_op jit(solution)/shard_map/all_to_all | solution.py:12
  55.5 2.6 %collective-permute-start.1 = (bf16[192,512]{1,0:T(8,128)(2,1)S(1)}, bf16[192,512]{1,0:T(8,128)(2,1)S(1)}, u32[]{:S(2)}, u32[]{:S(2)}) collective-permute-start(bf16[192,512]{1,0:T(8,128)(2,1)S(1)} %pad_maximum_fusion.3), channel_id=1, source_target_pairs={{8,0},{16,8},{24,16},{32,24},{40,32},{48,40},{56,48},{64,56},{72,6... | collective-permute-start | bytes 589832 | tf_op jit(solution)/shard_map/ppermute | solution.py:40
  58.0 3.0 %collective-permute-start = (bf16[192,512]{1,0:T(8,128)(2,1)S(1)}, bf16[192,512]{1,0:T(8,128)(2,1)S(1)}, u32[]{:S(2)}, u32[]{:S(2)}) collective-permute-start(bf16[192,512]{1,0:T(8,128)(2,1)S(1)} %pad_maximum_fusion.3), channel_id=1, source_target_pairs={{0,8},{8,16},{16,24},{24,32},{32,40},{40,48},{48,56},{56,64},{64,7... | collective-permute-start | bytes 589832 | tf_op jit(solution)/shard_map/ppermute | solution.py:39
  61.0 1.4 collective-permute-done.1
  67.5 3.5 %all-to-all-start.3 = ((bf16[4,7,48,256]{3,2,1,0:T(8,128)(2,1)}), bf16[4,7,48,256]{3,2,1,0:T(8,128)(2,1)S(1)}, u32[]{:S(2)}, u32[]{:S(2)}) async-start(bf16[4,7,48,256]{3,2,1,0:T(8,128)(2,1)} %copy.39), calls=%async_computation.3 | async-start | bytes 1376256 | tf_op jit(solution)/shard_map/all_to_all | solution.py:76
  71.0 1.9 %collective-permute-start.3 = (f32[2,512]{1,0:T(2,128)S(1)}, f32[2,512]{1,0:T(2,128)S(1)}, u32[]{:S(2)}, u32[]{:S(2)}) collective-permute-start(f32[2,512]{1,0:T(2,128)S(1)} %pad_maximum_fusion.6), channel_id=1, source_target_pairs={{8,0},{16,8},{24,16},{32,24},{40,32},{48,40},{56,48},{64,56},{72,6... | collective-permute-start | bytes 12296 | tf_op jit(solution)/shard_map/ppermute | solution.py:40
  73.0 4.4 %collective-permute-start.2 = (f32[2,512]{1,0:T(2,128)S(1)}, f32[2,512]{1,0:T(2,128)S(1)}, u32[]{:S(2)}, u32[]{:S(2)}) collective-permute-start(f32[2,512]{1,0:T(2,128)S(1)} %pad_maximum_fusion.6), channel_id=1, source_target_pairs={{0,8},{8,16},{16,24},{24,32},{32,40},{40,48},{48,56},{56,64},{64,7... | collective-permute-start | bytes 12296 | tf_op jit(solution)/shard_map/ppermute | solution.py:39
  78.3 7.6 %all-to-all-done.3 = bf16[4,7,48,256]{3,2,1,0:T(8,128)(2,1)S(1)} async-done(((bf16[4,7,48,256]{3,2,1,0:T(8,128)(2,1)}), bf16[4,7,48,256]{3,2,1,0:T(8,128)(2,1)S(1)}, u32[]{:S(2)}, u32[]{:S(2)}) %all-to-all-start.3) | async-done | bytes 688160 | tf_op jit(solution)/shard_map/all_to_all | solution.py:76
  85.9 3.5 %all-to-all-start.4 = ((bf16[4,7,48,256]{3,2,1,0:T(8,128)(2,1)}), bf16[4,7,48,256]{3,2,1,0:T(8,128)(2,1)S(1)}, u32[]{:S(2)}, u32[]{:S(2)}) async-start(bf16[4,7,48,256]{3,2,1,0:T(8,128)(2,1)} %copy.40), calls=%async_computation.4 | async-start | bytes 1376256 | tf_op jit(solution)/shard_map/all_to_all | solution.py:76
  89.4 17.6 %all-to-all-done.4 = bf16[4,7,48,256]{3,2,1,0:T(8,128)(2,1)S(1)} async-done(((bf16[4,7,48,256]{3,2,1,0:T(8,128)(2,1)}), bf16[4,7,48,256]{3,2,1,0:T(8,128)(2,1)S(1)}, u32[]{:S(2)}, u32[]{:S(2)}) %all-to-all-start.4) | async-done | bytes 688160 | tf_op jit(solution)/shard_map/all_to_all | solution.py:76
  107.3 3.2 %fusion.10 = (bf16[384,1536]{1,0:T(8,128)(2,1)}, bf16[384,1536]{1,0:T(8,128)(2,1)}) fusion(bf16[384,3072]{1,0:T(8,128)(2,1)} %all-gather.2.cloned.1.call-done), kind=kLoop, calls=%fused_computation.43 | loop fusion | bytes 4718592 | tf_op jit(solution)/shard_map/slice | solution.py:49
  111.7 12.9 %while.13 = (s32[]{:T(128)}, bf16[7,384,256]{1,2,0:T(8,128)(2,1)}, f32[7,256]{1,0:T(8,128)S(1)}, f32[]{:T(128)}, bf16[7,384,256]{2,1,0:T(8,128)(2,1)S(1)}, /*ind...) while((s32[]{:T(128)}, bf16[7,384,256]{1,2,0:T(8,128)(2,1)}, ...), condition=%wide.region_9.10_spmd, body=%wide.region_8.9_spmd.sunk | while | flops 2119975168 | bytes 8799963 | solution.py:111
  112.5 5.6 %fusion.21 = bf16[7,384,256]{1,2,0:T(8,128)(2,1)} fusion(bf16[7,384,256]{1,2,0:T(8,128)(2,1)} %get-tuple-element.341, s32[]{:T(128)S(6)} %select_n.31, bf16[7,384,128]{1,2,0:T(8,128)(2,1)S(1)} %copy.62, bf16[384,1536]{1,0:T(8,128)(2,1)} %get-tuple-element.364, f32[128,1536]{1,0:T(8,128)S(1)} %multiply_multiply_fusion.2, ...), kind=kOutput, calls=%fused_computation.4.clone.1 | convolution fusion | flops 2118402048 | bytes 5215744 | tf_op jit(solution)/shard_map/while/body/eval_jaxpr/ltj,mj->lmt/dot_general | solution.py:102
  119.0 5.6 %fusion.21 = bf16[7,384,256]{1,2,0:T(8,128)(2,1)} fusion(bf16[7,384,256]{1,2,0:T(8,128)(2,1)} %get-tuple-element.341, s32[]{:T(128)S(6)} %select_n.31, bf16[7,384,128]{1,2,0:T(8,128)(2,1)S(1)} %copy.62, bf16[384,1536]{1,0:T(8,128)(2,1)} %get-tuple-element.364, f32[128,1536]{1,0:T(8,128)S(1)} %multiply_multiply_fusion.2, ...), kind=kOutput, calls=%fused_computation.4.clone.1 | convolution fusion | flops 2118402048 | bytes 5215744 | tf_op jit(solution)/shard_map/while/body/eval_jaxpr/ltj,mj->lmt/dot_general | solution.py:102
  124.6 2.3 %copy.44 = bf16[7,384,256]{2,0,1:T(8,128)(2,1)S(1)} copy(bf16[7,384,256]{1,2,0:T(8,128)(2,1)} %get-tuple-element.171) | data formatting | bytes 2752512 | tf_op jit(solution)/shard_map/while | solution.py:111
  126.9 22.3 %all_to_all.47 = bf16[7,384,256]{2,0,1:T(8,128)(2,1)S(1)} all-to-all(bf16[7,384,256]{2,0,1:T(8,128)(2,1)S(1)} %copy.44), channel_id=1, replica_groups=mesh['region'=16,'depth'=2,'member'=4] {'member'}, dimensions={1} | all-to-all | bytes 2752512 | tf_op jit(solution)/shard_map/all_to_all | solution.py:167
  150.4 1.8 %all_to_all.38 = bf16[7,96,1024]{2,1,0:T(8,128)(2,1)} reshape(bf16[7,96,4,256]{3,2,1,0:T(4,128)(2,1)S(1)} %copy.46) | data formatting | bytes 2752512 | tf_op jit(solution)/shard_map/all_to_all | solution.py:167
  (69 shorter events, 16.2 us)
Async XLA Ops:
  7.2 9.3 %copy-start = (f32[7]{0:T(128)S(1)}, f32[7]{0:T(128)}, u32[]{:S(2)}) copy-start(f32[7]{0:T(128)} %param.9) | copy-start | bytes 88
  16.4 6.6 %copy-start.1 = (bf16[7,96,1024]{2,1,0:T(8,128)(2,1)S(1)}, bf16[7,96,1024]{2,1,0:T(8,128)(2,1)}, u32[]{:S(2)}) copy-start(bf16[7,96,1024]{2,1,0:T(8,128)(2,1)} %param.8) | copy-start | bytes 4128772
  17.9 10.2 %all-to-all-start = ((bf16[2,96,512]{2,1,0:T(8,128)(2,1)}), bf16[2,96,512]{2,1,0:T(8,128)(2,1)S(1)}, u32[]{:S(2)}, u32[]{:S(2)}) async-start(bf16[2,96,512]{2,1,0:T(8,128)(2,1)} %broadcast_in_dim.41), calls=%async_computation | async-start | bytes 393216 | tf_op jit(solution)/shard_map/all_to_all | solution.py:12
  22.9 14.1 %copy-start.3 = (f32[512]{0:T(512)S(1)}, f32[512]{0:T(512)}, u32[]{:S(2)}) copy-start(f32[512]{0:T(512)} %param.12) | copy-start | bytes 6148
  22.9 14.1 %copy-start.4 = (f32[512]{0:T(512)S(1)}, f32[512]{0:T(512)}, u32[]{:S(2)}) copy-start(f32[512]{0:T(512)} %param.11) | copy-start | bytes 6148
  22.9 32.4 %copy-start.2 = (f32[96,512]{1,0:T(8,128)S(1)}, f32[96,512]{1,0:T(8,128)}, u32[]{:S(2)}) copy-start(f32[96,512]{1,0:T(8,128)} %param.13) | copy-start | bytes 589828
  22.9 84.4 %all-gather.2.cloned.1.call-start = ((), (), s32[]{:S(2)}) async-start(), calls=%async_computation.6 | async-start | bytes 2949120 | tf_op jit(solution)/shard_map/all_gather | solution.py:47
  55.5 7.0 %collective-permute-start.1 = (bf16[192,512]{1,0:T(8,128)(2,1)S(1)}, bf16[192,512]{1,0:T(8,128)(2,1)S(1)}, u32[]{:S(2)}, u32[]{:S(2)}) collective-permute-start(bf16[192,512]{1,0:T(8,128)(2,1)S(1)} %pad_maximum_fusion.3), channel_id=1, source_target_pairs={{8,0},{16,8},{24,16},{32,24},{40,32},{48,40},{56,48},{64,56},{72,6... | collective-permute-start | bytes 589832 | tf_op jit(solution)/shard_map/ppermute | solution.py:40
  58.0 5.6 %collective-permute-start = (bf16[192,512]{1,0:T(8,128)(2,1)S(1)}, bf16[192,512]{1,0:T(8,128)(2,1)S(1)}, u32[]{:S(2)}, u32[]{:S(2)}) collective-permute-start(bf16[192,512]{1,0:T(8,128)(2,1)S(1)} %pad_maximum_fusion.3), channel_id=1, source_target_pairs={{0,8},{8,16},{16,24},{24,32},{32,40},{40,48},{48,56},{56,64},{64,7... | collective-permute-start | bytes 589832 | tf_op jit(solution)/shard_map/ppermute | solution.py:39
  67.5 18.4 %all-to-all-start.3 = ((bf16[4,7,48,256]{3,2,1,0:T(8,128)(2,1)}), bf16[4,7,48,256]{3,2,1,0:T(8,128)(2,1)S(1)}, u32[]{:S(2)}, u32[]{:S(2)}) async-start(bf16[4,7,48,256]{3,2,1,0:T(8,128)(2,1)} %copy.39), calls=%async_computation.3 | async-start | bytes 1376256 | tf_op jit(solution)/shard_map/all_to_all | solution.py:76
  71.0 18.3 %collective-permute-start.3 = (f32[2,512]{1,0:T(2,128)S(1)}, f32[2,512]{1,0:T(2,128)S(1)}, u32[]{:S(2)}, u32[]{:S(2)}) collective-permute-start(f32[2,512]{1,0:T(2,128)S(1)} %pad_maximum_fusion.6), channel_id=1, source_target_pairs={{8,0},{16,8},{24,16},{32,24},{40,32},{48,40},{56,48},{64,56},{72,6... | collective-permute-start | bytes 12296 | tf_op jit(solution)/shard_map/ppermute | solution.py:40
  73.0 16.4 %collective-permute-start.2 = (f32[2,512]{1,0:T(2,128)S(1)}, f32[2,512]{1,0:T(2,128)S(1)}, u32[]{:S(2)}, u32[]{:S(2)}) collective-permute-start(f32[2,512]{1,0:T(2,128)S(1)} %pad_maximum_fusion.6), channel_id=1, source_target_pairs={{0,8},{8,16},{16,24},{24,32},{32,40},{40,48},{48,56},{56,64},{64,7... | collective-permute-start | bytes 12296 | tf_op jit(solution)/shard_map/ppermute | solution.py:39
  85.9 21.1 %all-to-all-start.4 = ((bf16[4,7,48,256]{3,2,1,0:T(8,128)(2,1)}), bf16[4,7,48,256]{3,2,1,0:T(8,128)(2,1)S(1)}, u32[]{:S(2)}, u32[]{:S(2)}) async-start(bf16[4,7,48,256]{3,2,1,0:T(8,128)(2,1)} %copy.40), calls=%async_computation.4 | async-start | bytes 1376256 | tf_op jit(solution)/shard_map/all_to_all | solution.py:76
Sparse Core Ops, SparseCore 0:
  64.7 42.5 all-gather.1
where the time goes:
time: 162 us; the launch traced here: 160 us
  blocking collectives  45.2 us (28%)
  waiting for transfers between devices  32.6 us (20%)
  starting transfers between devices  23.9 us (15%)
  local copies, waits for them, and re-layouts  21.7 us (13%)
  between operations  16.9 us (10%)
  matrix products  12 us (7%)
  other arithmetic  7.83 us (5%)
    all_to_all x2, waiting for transfers between devices, exchange_in_pieces(): lax.all_to_all(section, axis, split_axis=0, concat_axis=0, tiled=True)  25.1 us
    all_to_all x2, blocking collectives, sent_to_all(): return lax.all_to_all(copies, axis, split_axis=0, concat_axis=0, tiled=True)  22.9 us
    all_to_all x1, blocking collectives, shards(): lax.all_to_all(updated, 'member', split_axis=1, concat_axis=2, tiled=True)  22.3 us
    dot_general x2, matrix products, one_block(): jnp.einsum('ltj,mj->lmt', kalman_gain, perturbed, preferred_element_type=...  11.2 us
    ppermute x2, starting transfers between devices, extended(): before = lax.ppermute(last, axis, up)  7.38 us
    all_to_all x2, starting transfers between devices, exchange_in_pieces(): lax.all_to_all(section, axis, split_axis=0, concat_axis=0, tiled=True)  6.98 us
    all_to_all x1, starting transfers between devices, sent_to_all(): return lax.all_to_all(copies, axis, split_axis=0, concat_axis=0, tiled=True)  5 us
    all_to_all x1, waiting for transfers between devices, sent_to_all(): return lax.all_to_all(copies, axis, split_axis=0, concat_axis=0, tiled=True)  4.82 us
  transfers between devices with their start and end apart: 8, of which 5 were waited for; matrix products, arithmetic and copies ran while one was open for 3% of the time, Pallas kernels for 0%

commit v1 on v0

v1 whole, which is shorter than its diff:
```python
import jax
import jax.numpy as jnp
from jax import lax
from jax.experimental import pallas as pl
from jax.experimental.pallas import tpu as pltpu
from jax.sharding import PartitionSpec as P

MEMBERS = 384
RADIUS = 1024.0
MESH = pl.DeviceIdType.MESH
F32 = jnp.float32
BF16 = jnp.bfloat16


def dot(a, b):
    return lax.dot_general(a, b, (((1,), (0,)), ((), ())), preferred_element_type=F32)


def kernel(
    regions,
    peers,
    ens_hbm,
    wts_hbm,
    tiles_hbm,
    vals_hbm,
    err_hbm,
    noise_hbm,
    out_hbm,
    infl_ref,
    ens,
    wts,
    small,
    noise,
    blend,
    hot,
    part,
    obs,
    slots,
    recv,
    hold,
    back,
    back_hold,
    anom_t,
    taper,
    gain,
    pert,
    tot,
    load_sem,
    e_send,
    e_recv,
    b_send,
    b_recv,
    o_send,
    o_recv,
    n_send,
    n_recv,
    s_send,
    s_recv,
    d_send,
    d_recv,
    i_send,
    i_recv,
    own_sem,
    out_sem,
):
    n_var, own, n_tile = ens.shape
    n_obs = noise.shape[1]
    half = own // 2
    share = n_tile // peers
    r = lax.axis_index("region")
    d = lax.axis_index("depth")
    j = lax.axis_index("member")
    right, left, opp = lax.rem(j + 1, peers), lax.rem(j + 3, peers), lax.rem(j + 2, peers)
    after, before = lax.rem(r + 1, regions), lax.rem(r + regions - 1, regions)

    def rows(b, start=0, count=None):
        return pl.ds(pl.multiple_of(b * own + start, 16), own if count is None else count)

    def cols(b):
        return pl.ds(pl.multiple_of(b * share, 128), share)

    def remote(src, dst, send, rec, **where):
        return pltpu.make_async_remote_copy(src, dst, send, rec, device_id=where, device_id_type=MESH)

    loads = [
        pltpu.make_async_copy(noise_hbm, noise, load_sem.at[0]),
        pltpu.make_async_copy(err_hbm, small.at[1, pl.ds(2, 1)], load_sem.at[1]),
        pltpu.make_async_copy(tiles_hbm, small.at[1, pl.ds(0, 1)], load_sem.at[2]),
        pltpu.make_async_copy(vals_hbm, small.at[1, pl.ds(1, 1)], load_sem.at[3]),
        pltpu.make_async_copy(wts_hbm, wts, load_sem.at[4]),
        pltpu.make_async_copy(ens_hbm, ens, load_sem.at[5]),
    ]
    for copy in loads:
        copy.start()

    def take_own(l):
        return pltpu.make_async_copy(ens_hbm.at[l, :, cols(j)], recv.at[l, rows(j), :], own_sem.at[l])

    lax.fori_loop(0, n_var, lambda l, c: (take_own(l).start(), c)[1], 0)

    barrier = pltpu.get_barrier_semaphore()
    pl.semaphore_signal(barrier, inc=1, device_id={"member": right}, device_id_type=MESH)
    pl.semaphore_signal(barrier, inc=1, device_id={"member": left}, device_id_type=MESH)
    pl.semaphore_signal(barrier, inc=1, device_id={"depth": 1 - d}, device_id_type=MESH)

    def greet(o, c):
        pl.semaphore_signal(barrier, inc=1, device_id={"region": lax.rem(r + o, regions)}, device_id_type=MESH)
        return c

    lax.fori_loop(1, regions, greet, 0)

    for copy in loads[:4]:
        copy.wait()
    obs[1, 0, rows(j), :] = (jnp.sqrt(small[1, 2:3, :]) * noise[...]).astype(BF16)
    loads[4].wait()
    loads[5].wait()
    pl.semaphore_wait(barrier, regions + 2)

    def e_copies(l):
        return (
            remote(ens.at[l, pl.ds(0, half), cols(opp)], hold.at[0, l], e_send.at[2], e_recv.at[2, l], member=right),
            remote(ens.at[l, pl.ds(half, half), cols(opp)], hold.at[1, l], e_send.at[3], e_recv.at[3, l], member=left),
            remote(ens.at[l, :, cols(right)], recv.at[l, rows(j), :], e_send.at[0], e_recv.at[0, l], member=right),
            remote(ens.at[l, :, cols(left)], recv.at[l, rows(j), :], e_send.at[1], e_recv.at[1, l], member=left),
        )

    def e_relays(l):
        return (
            remote(hold.at[0, l], recv.at[l, rows(left, 0, half), :], e_send.at[4], e_recv.at[4, l], member=right),
            remote(hold.at[1, l], recv.at[l, rows(right, half, half), :], e_send.at[5], e_recv.at[5, l], member=left),
        )

    def send_ens(first, last):
        def body(l, c):
            for copy in e_copies(l):
                copy.start()
            return c

        lax.fori_loop(first, last, body, 0)

    def relay_ens(l):
        held, fwd = e_copies(l), e_relays(l)
        held[0].wait_recv()
        fwd[0].start()
        held[1].wait_recv()
        fwd[1].start()

    def take_ens(l):
        copies, fwd = e_copies(l), e_relays(l)
        take_own(l).wait()
        copies[2].wait_recv()
        copies[3].wait_recv()
        fwd[0].wait_recv()
        fwd[1].wait_recv()

    def o_copies(q):
        block = obs.at[1, q, rows(j), :]
        return (
            remote(block, block, o_send.at[q, 0], o_recv.at[q, 0], member=right),
            remote(block, block, o_send.at[q, 1], o_recv.at[q, 1], member=left),
        )

    def o_relays(q):
        top, low = obs.at[1, q, rows(left, 0, half), :], obs.at[1, q, rows(right, half, half), :]
        return (
            remote(top, top, o_send.at[q, 2], o_recv.at[q, 2], member=right),
            remote(low, low, o_send.at[q, 3], o_recv.at[q, 3], member=left),
        )

    def to_beside(q, b):
        block = obs.at[1, q, rows(b), :]
        remote(block, obs.at[0, q, rows(b), :], n_send.at[q, 0], n_recv.at[q, 0], region=after).start()
        remote(block, obs.at[2, q, rows(b), :], n_send.at[q, 1], n_recv.at[q, 1], region=before).start()

    def from_beside(q):
        return (
            remote(obs.at[1, q], obs.at[0, q], n_send.at[q, 0], n_recv.at[q, 0], region=after),
            remote(obs.at[1, q], obs.at[2, q], n_send.at[q, 1], n_recv.at[q, 1], region=before),
        )

    small_copies = (
        remote(small.at[1], small.at[0], s_send.at[0], s_recv.at[0], region=after),
        remote(small.at[1], small.at[2], s_send.at[1], s_recv.at[1], region=before),
    )

    def spread_block(q, relay):
        for k, copy in enumerate(o_copies(q)):
            copy.wait_recv()
            o_relays(q)[k].start()
        to_beside(q, left)
        to_beside(q, right)

    def finish_block(q):
        for copy in o_relays(q):
            copy.wait_recv()
        to_beside(q, opp)

    send_ens(0, 3)
    for copy in small_copies:
        copy.start()
    to_beside(0, j)
    for copy in o_copies(0):
        copy.start()

    def blended(i, c):
        at = pl.ds(pl.multiple_of(i * 16, 16), 16)
        total = wts[0] * ens[0, at, :].astype(F32)
        for l in range(1, n_var):
            total = total + wts[l] * ens[l, at, :].astype(F32)
        blend[at, :] = total.astype(BF16)
        return c

    lax.fori_loop(0, own // 16, blended, 0)
    tile_row = small[1, 0:1, :]

    def one_hot(i, c):
        at = pl.ds(pl.multiple_of(i * 128, 128), 128)
        index = (lax.broadcasted_iota(jnp.int32, (128, n_obs), 0) + i * 128).astype(F32)
        hot[at, :] = jnp.where(index == tile_row, 1.0, 0.0).astype(BF16)
        return c

    lax.fori_loop(0, n_tile // 128, one_hot, 0)
    part[0] = dot(blend[...], hot[...]).astype(BF16)
    swap = remote(part.at[0], part.at[1], d_send, d_recv, depth=1 - d)
    swap.start()

    relay_ens(0)
    relay_ens(1)
    swap.wait_recv()
    obs[1, 1, rows(j), :] = (part[0].astype(F32) + part[1].astype(F32)).astype(BF16)
    for copy in o_copies(1):
        copy.start()
    to_beside(1, j)
    send_ens(3, 4)
    relay_ens(2)
    spread_block(0, None)
    spread_block(1, None)
    send_ens(4, 7)
    finish_block(0)
    relay_ens(3)
    finish_block(1)

    def stats(w):
        pred = obs[w, 1].astype(F32)
        mean = jnp.sum(pred, axis=0, keepdims=True) / MEMBERS
        dev = pred - mean
        spread = jnp.sum(dev * dev, axis=0, keepdims=True) / (MEMBERS - 1)
        tot[w, 0:1, :] = mean
        tot[w, 1:2, :] = spread
        anom_t[pl.ds(w * n_obs, n_obs), :] = dev.T.astype(BF16)
        return small[w, 1:2, :] - mean, spread

    innovation, spread = stats(1)
    squares = jnp.sum(innovation * innovation, axis=1, keepdims=True)
    widths = jnp.sum(spread + small[1, 2:3, :], axis=1, keepdims=True)
    line = lax.broadcasted_iota(jnp.int32, (8, 128), 0)
    slots[r] = jnp.where(line < 4, squares, widths)

    def tell(o, c):
        remote(slots.at[r], slots.at[r], i_send, i_recv, region=lax.rem(r + o, regions)).start()
        return c

    lax.fori_loop(1, regions, tell, 0)

    for copy in small_copies:
        copy.wait_recv()
    lane = lax.broadcasted_iota(jnp.int32, (n_obs, 128), 1) + j * share
    shifts = (
        jnp.where(r == 0, -16.0 * RADIUS, -RADIUS),
        jnp.float32(0.0),
        jnp.where(r == regions - 1, 16.0 * RADIUS, RADIUS),
    )
    for w in range(3):
        spot = jnp.broadcast_to(small[w, 0:1, :] + shifts[w], (128, n_obs)).T
        for c in range(share // 128):
            near = jnp.maximum(0.0, 1.0 - jnp.abs((lane + c * 128).astype(F32) - spot) / RADIUS)
            taper[pl.ds(w * n_obs, n_obs), pl.ds(c * 128, 128)] = near * near / (MEMBERS - 1)

    relay_ens(4)
    for q in range(2):
        for copy in from_beside(q):
            copy.wait_recv()
    stats(0)
    stats(2)

    remote(slots.at[pl.ds(0, regions - 1)], slots.at[pl.ds(1, regions - 1)], i_send, i_recv, region=after).wait_recv()
    total = jnp.sum(slots[...], axis=0)
    infl = total[0:1, 0:1] / total[4:5, 0:1]
    root = jnp.sqrt(infl)
    infl_ref[0, 0] = infl[0, 0]

    for w in range(3):
        mean, spread = tot[w, 0:1, :], tot[w, 1:2, :]
        factor = infl / (infl * spread + small[w, 2:3, :])
        innovation = small[w, 1:2, :] - mean
        dev = obs[w, 1].astype(F32) - mean
        moved = innovation + obs[w, 0].astype(F32) - root * dev
        pert[:, pl.ds(w * n_obs, n_obs)] = (moved * factor).astype(BF16)

    def b_copies(l):
        return (
            remote(back.at[l, rows(opp, 0, half), :], back_hold.at[0, l], b_send.at[2], b_recv.at[2, l], member=right),
            remote(back.at[l, rows(opp, half, half), :], back_hold.at[1, l], b_send.at[3], b_recv.at[3, l], member=left),
            remote(back.at[l, rows(right), :], out_hbm.at[l, :, cols(j)], b_send.at[0], b_recv.at[0, l], member=right),
            remote(back.at[l, rows(left), :], out_hbm.at[l, :, cols(j)], b_send.at[1], b_recv.at[1, l], member=left),
        )

    def b_relays(l):
        return (
            remote(back_hold.at[0, l], out_hbm.at[l, pl.ds(0, half), cols(left)], b_send.at[4], b_recv.at[4, l], member=right),
            remote(back_hold.at[1, l], out_hbm.at[l, pl.ds(half, half), cols(right)], b_send.at[5], b_recv.at[5, l], member=left),
        )

    def keep(l):
        return pltpu.make_async_copy(back.at[l, rows(j), :], out_hbm.at[l, :, cols(j)], out_sem.at[l])

    def relay_back(l):
        held, fwd = b_copies(l), b_relays(l)
        held[0].wait_recv()
        fwd[0].start()
        held[1].wait_recv()
        fwd[1].start()

    def analyse(l, c):
        @pl.when(l < 2)
        def _():
            relay_ens(l + 5)

        take_ens(l)
        state = recv[l].astype(F32)
        mean = jnp.sum(state, axis=0, keepdims=True) / MEMBERS
        anom = (state - mean).astype(BF16)
        for w in range(3):
            at = pl.ds(w * n_obs, n_obs)
            gain[at, :] = (dot(anom_t[at, :], anom) * taper[at, :]).astype(BF16)
        increment = dot(pert[...], gain[...])
        back[l] = (mean + root * anom.astype(F32) + increment).astype(BF16)
        for copy in b_copies(l):
            copy.start()
        keep(l).start()

        @pl.when(l > 0)
        def _():
            relay_back(l - 1)

        return c

    lax.fori_loop(0, n_var, analyse, 0)
    relay_back(n_var - 1)

    def finish(l, c):
        copies, fwd = b_copies(l), b_relays(l)
        keep(l).wait()
        copies[2].wait_recv()
        copies[3].wait_recv()
        fwd[0].wait_recv()
        fwd[1].wait_recv()
        return c

    lax.fori_loop(0, n_var, finish, 0)

    whole, part_of = recv.at[:, pl.ds(0, own), :], hold.at[0]
    for sems in (e_send, b_send):
        for k in range(6):
            block = whole if k < 2 else part_of
            remote(block, block, sems.at[k], e_recv.at[0, 0], member=right).wait_send()
    for q in range(2):
        for copy in o_copies(q) + o_relays(q) + from_beside(q):
            copy.wait_send()
    for copy in small_copies:
        copy.wait_send()
    swap.wait_send()
    remote(slots.at[pl.ds(0, regions - 1)], slots.at[pl.ds(1, regions - 1)], i_send, i_recv, region=after).wait_send()


def solution(mesh):
    regions, peers = mesh.shape["region"], mesh.shape["member"]

    def shards(ensemble, obs_weights, obs_tiles, obs_values, obs_error, obs_noise):
        n_var, own, n_tile = ensemble.shape
        n_obs = obs_tiles.shape[0]
        share, members = n_tile // peers, own * peers
        DMA = pltpu.SemaphoreType.DMA
        scratch = [
            pltpu.VMEM((n_var, own, n_tile), BF16),
            pltpu.SMEM((n_var,), F32),
            pltpu.VMEM((3, 8, n_obs), F32),
            pltpu.VMEM((own, n_obs), F32),
            pltpu.VMEM((own, n_tile), BF16),
            pltpu.VMEM((n_tile, n_obs), BF16),
            pltpu.VMEM((2, own, n_obs), BF16),
            pltpu.VMEM((3, 2, members, n_obs), BF16),
            pltpu.VMEM((regions, 8, 128), F32),
            pltpu.VMEM((n_var, members, share), BF16),
            pltpu.VMEM((2, n_var, own // 2, share), BF16),
            pltpu.VMEM((n_var, members, share), BF16),
            pltpu.VMEM((2, n_var, own // 2, share), BF16),
            pltpu.VMEM((3 * n_obs, members), BF16),
            pltpu.VMEM((3 * n_obs, share), F32),
            pltpu.VMEM((3 * n_obs, share), BF16),
            pltpu.VMEM((members, 3 * n_obs), BF16),
            pltpu.VMEM((3, 8, n_obs), F32),
            DMA((6,)),
            DMA((6,)),
            DMA((6, n_var)),
            DMA((6,)),
            DMA((6, n_var)),
            DMA((2, 4)),
            DMA((2, 4)),
            DMA((2, 2)),
            DMA((2, 2)),
            DMA((2,)),
            DMA((2,)),
            DMA,
            DMA,
            DMA,
            DMA,
            DMA((n_var,)),
            DMA((n_var,)),
        ]
        hbm = pl.BlockSpec(memory_space=pl.ANY)
        analysis, inflation = pl.pallas_call(
            lambda *refs: kernel(regions, peers, *refs),
            out_shape=(
                jax.ShapeDtypeStruct(ensemble.shape, BF16),
                jax.ShapeDtypeStruct((1, 1), F32),
            ),
            in_specs=[hbm] * 6,
            out_specs=(hbm, pl.BlockSpec(memory_space=pltpu.SMEM)),
            scratch_shapes=scratch,
            compiler_params=pltpu.CompilerParams(
                collective_id=0, has_side_effects=True, vmem_limit_bytes=56 * 2**20
            ),
        )(
            ensemble,
            obs_weights,
            obs_tiles.astype(F32).reshape(1, n_obs),
            obs_values.reshape(1, n_obs),
            obs_error.reshape(1, n_obs),
            obs_noise,
        )
        return analysis, inflation.reshape(())

    return jax.shard_map(
        shards,
        mesh=mesh,
        in_specs=(
            P("depth", "member", "region"),
            P("depth"),
            P("region"),
            P("region"),
            P("region"),
            P("member", "region"),
        ),
        out_specs=(P("depth", "member", "region"), P()),
        check_vma=False,
    )
```

time: 162 us -> 58.5 us (0.36)
  the two profiles are of different devices: /device:TPU:1 before, /device:TPU:2 now
where the time goes in v1:
time: 58.5 us; the launch traced here: 58.3 us
  Pallas kernels  52.1 us (89%)
  local copies, waits for them, and re-layouts  2.56 us (4%)
  between operations  2.4 us (4%)
  other arithmetic  1.26 us (2%)
    pallas_call x1, Pallas kernels, shards(): pl.pallas_call(lambda *refs: kernel(regions, peers, *refs), out_shape=(ja...  52.1 us
    unnamed x1, local copies, waits for them, and re-layouts  2.56 us
    convert_element_type x1, other arithmetic, shards(): obs_tiles.astype(F32).reshape(1, n_obs)  1.26 us

profile of v1, /device:TPU:2, one launch (start us, length us, event | category | flops | bytes accessed | tf_op | source)
XLA Modules:
  0.0 58.3 jit_solution(5937791046407815005)
XLA Ops:
  0.6 1.3 %convert_element_type.3 = f32[512]{0:T(512)} convert(s32[512]{0:T(512)} %param.8) | non-fusion elementwise | flops 512 | bytes 4096 | tf_op jit(solution)/shard_map/convert_element_type | solution.py:437
  1.9 52.1 %shard_map.77 = (bf16[7,96,1024]{2,1,0:T(8,128)(2,1)}, f32[1,1]{1,0:T(1,128)}) custom-call(bf16[7,96,1024]{2,1,0:T(8,128)(2,1)} %refs_0_.1, f32[7]{0:T(128)} %refs_1_.1, f32[1,512]{1,0:T(1,128)} %bitcast.4, f32[1,512]{1,0:T(1,128)} %bitcast.5, f32[1,512]{1,0:T(1,128)} %bitcast.6, f32[96,512]{1,0:T(8,128)} %refs_5_.1), custom_call_target="tpu_custom_call" | custom-call | tf_op jit(solution)/shard_map/pallas_call | solution.py:422
  54.0 2.6 %copy.10 = bf16[7,96,1024]{2,1,0:T(8,128)(2,1)} copy(bf16[7,96,1024]{2,1,0:T(8,128)(2,1)} %get-tuple-element.8) | data formatting | bytes 2752512

commit v2 on v1

v2 whole, which is shorter than its diff:
```python
import jax
import jax.numpy as jnp
from jax import lax
from jax.experimental import pallas as pl
from jax.experimental.pallas import tpu as pltpu
from jax.sharding import PartitionSpec as P

MEMBERS = 384
RADIUS = 1024.0
MESH = pl.DeviceIdType.MESH
F32 = jnp.float32
BF16 = jnp.bfloat16


def dot(a, b):
    return lax.dot_general(a, b, (((1,), (0,)), ((), ())), preferred_element_type=F32)


def kernel(
    regions,
    peers,
    ens_hbm,
    wts_hbm,
    tiles_hbm,
    vals_hbm,
    err_hbm,
    noise_hbm,
    out,
    infl_ref,
    ens,
    wts,
    spots,
    small,
    noise,
    blend,
    hot,
    part,
    obs,
    slots,
    recv,
    back,
    anoms,
    means,
    anom_t,
    taper,
    gain,
    pert,
    tot,
    load_sem,
    e_send,
    e_recv,
    b_send,
    b_recv,
    o_send,
    o_recv,
    y_send,
    y_recv,
    n_send,
    n_recv,
    s_send,
    s_recv,
    d_send,
    d_recv,
    i_send,
    i_recv,
    own_sem,
):
    n_var, own, n_tile = ens.shape
    n_obs = noise.shape[1]
    share = n_tile // peers
    r = lax.axis_index("region")
    d = lax.axis_index("depth")
    j = lax.axis_index("member")
    right, left, opp = lax.rem(j + 1, peers), lax.rem(j + 3, peers), lax.rem(j + 2, peers)
    after, before = lax.rem(r + 1, regions), lax.rem(r + regions - 1, regions)
    others = (opp, right, left)

    def rows(b):
        return pl.ds(pl.multiple_of(b * own, 16), own)

    def cols(b):
        return pl.ds(pl.multiple_of(b * share, 128), share)

    def half(h):
        return pl.ds(pl.multiple_of(h * (n_obs // 2), 128), n_obs // 2)

    def remote(src, dst, send, rec, **where):
        return pltpu.make_async_remote_copy(src, dst, send, rec, device_id=where, device_id_type=MESH)

    barrier = pltpu.get_barrier_semaphore()

    def greet(**where):
        pl.semaphore_signal(barrier, inc=1, device_id=where, device_id_type=MESH)

    def greet_region(o, c):
        greet(region=lax.rem(r + o, regions))
        return c

    lax.fori_loop(1, regions, greet_region, 0)
    for p in others:
        greet(member=p)
    greet(depth=1 - d)

    loads = [
        pltpu.make_async_copy(ens_hbm, ens, load_sem.at[0]),
        pltpu.make_async_copy(wts_hbm, wts, load_sem.at[1]),
        pltpu.make_async_copy(tiles_hbm, spots, load_sem.at[2]),
        pltpu.make_async_copy(err_hbm, small.at[1, pl.ds(2, 1)], load_sem.at[3]),
        pltpu.make_async_copy(vals_hbm, small.at[1, pl.ds(1, 1)], load_sem.at[4]),
        pltpu.make_async_copy(noise_hbm, noise, load_sem.at[5]),
    ]
    for copy in loads:
        copy.start()

    def take_own(l):
        return pltpu.make_async_copy(ens_hbm.at[l, :, cols(j)], recv.at[l, rows(j), :], own_sem.at[l])

    lax.fori_loop(0, n_var, lambda l, c: (take_own(l).start(), c)[1], 0)

    def blended(i, c):
        at = pl.ds(pl.multiple_of(i * 16, 16), 16)
        total = wts[0] * ens[0, at, :].astype(F32)
        for l in range(1, n_var):
            total = total + wts[l] * ens[l, at, :].astype(F32)
        blend[at, :] = total.astype(BF16)
        return c

    with jax.named_scope("load_small"):
        loads[1].wait()
        loads[2].wait()
    tile_row = spots[...].astype(F32)
    small[1, 0:1, :] = tile_row

    def one_hot(i, c):
        at = pl.ds(pl.multiple_of(i * 128, 128), 128)
        index = (lax.broadcasted_iota(jnp.int32, (128, n_obs), 0) + i * 128).astype(F32)
        hot[at, :] = jnp.where(index == tile_row, 1.0, 0.0).astype(BF16)
        return c

    with jax.named_scope("hot"):
        lax.fori_loop(0, n_tile // 128, one_hot, 0)
    with jax.named_scope("noise"):
        for copy in loads[3:]:
            copy.wait()
        obs[1, 0, rows(j), :] = (jnp.sqrt(small[1, 2:3, :]) * noise[...]).astype(BF16)
    with jax.named_scope("blend"):
        loads[0].wait()
        lax.fori_loop(0, own // 16, blended, 0)
    with jax.named_scope("pick"):
        part[0] = dot(blend[...], hot[...]).astype(BF16)
    with jax.named_scope("barrier"):
        pl.semaphore_wait(barrier, regions + 3)

    def e_copies(l):
        return [
            remote(ens.at[l, :, cols(p)], recv.at[l, rows(j), :], e_send.at[k], e_recv.at[k, l], member=p)
            for k, p in enumerate(others)
        ]

    def send_ens(first, last):
        def body(l, c):
            for copy in e_copies(l):
                copy.start()
            return c

        lax.fori_loop(first, last, body, 0)

    def o_copies(q):
        block = obs.at[1, 1, rows(j), :] if q else obs.at[1, 0, rows(j), half(d)]
        return [
            remote(block, block, o_send.at[q, k], o_recv.at[q, k], member=p) for k, p in enumerate(others)
        ]

    def to_beside(q, b, h=None):
        at = (rows(b), slice(None)) if h is None else (rows(b), half(h))
        remote(obs.at[(1, q) + at], obs.at[(0, q) + at], n_send.at[q, 0], n_recv.at[q, 0], region=after).start()
        remote(obs.at[(1, q) + at], obs.at[(2, q) + at], n_send.at[q, 1], n_recv.at[q, 1], region=before).start()

    def from_beside(q):
        return (
            remote(obs.at[1, q], obs.at[0, q], n_send.at[q, 0], n_recv.at[q, 0], region=after),
            remote(obs.at[1, q], obs.at[2, q], n_send.at[q, 1], n_recv.at[q, 1], region=before),
        )

    def to_depth(b):
        block = obs.at[1, 0, rows(b), half(d)]
        remote(block, block, y_send, y_recv, depth=1 - d).start()

    three = obs.at[1, 0, pl.ds(0, 3 * own), half(d)]
    from_depth = remote(three, three, y_send, y_recv, depth=1 - d)
    small_copies = (
        remote(small.at[1], small.at[0], s_send.at[0], s_recv.at[0], region=after),
        remote(small.at[1], small.at[2], s_send.at[1], s_recv.at[1], region=before),
    )
    swap = remote(part.at[0], part.at[1], d_send, d_recv, depth=1 - d)

    swap.start()
    for copy in o_copies(0):
        copy.start()
    send_ens(0, 1)
    for copy in small_copies:
        copy.start()
    to_beside(0, j)

    with jax.named_scope("small"):
        for copy in small_copies:
            copy.wait_recv()
    lane = lax.broadcasted_iota(jnp.int32, (n_obs, 128), 1) + j * share
    shifts = (
        jnp.where(r == 0, -16.0 * RADIUS, -RADIUS),
        jnp.float32(0.0),
        jnp.where(r == regions - 1, 16.0 * RADIUS, RADIUS),
    )
    with jax.named_scope("taper"):
        for w in range(3):
            spot = jnp.broadcast_to(small[w, 0:1, :] + shifts[w], (128, n_obs)).T
            for c in range(share // 128):
                near = jnp.maximum(0.0, 1.0 - jnp.abs((lane + c * 128).astype(F32) - spot) / RADIUS)
                taper[pl.ds(w * n_obs, n_obs), pl.ds(c * 128, 128)] = near * near / (MEMBERS - 1)

    with jax.named_scope("swap"):
        swap.wait_recv()
    obs[1, 1, rows(j), :] = (part[0].astype(F32) + part[1].astype(F32)).astype(BF16)
    for copy in o_copies(1):
        copy.start()
    to_beside(1, j)
    send_ens(1, n_var)
    with jax.named_scope("noise_x"):
        for copy, b in zip(o_copies(0), (opp, left, right)):
            copy.wait_recv()
            to_depth(b)
            to_beside(0, b, d)
    with jax.named_scope("noise_y"):
        from_depth.wait_recv()
    for b in others:
        to_beside(0, b, 1 - d)
    with jax.named_scope("pred_x"):
        for k, b in ((2, right), (1, left), (0, opp)):
            o_copies(1)[k].wait_recv()
            to_beside(1, b)

    def stats(w):
        pred = obs[w, 1].astype(F32)
        mean = jnp.sum(pred, axis=0, keepdims=True) / MEMBERS
        dev = pred - mean
        spread = jnp.sum(dev * dev, axis=0, keepdims=True) / (MEMBERS - 1)
        tot[w, 0:1, :] = mean
        tot[w, 1:2, :] = spread
        anom_t[pl.ds(w * n_obs, n_obs), :] = dev.T.astype(BF16)
        return small[w, 1:2, :] - mean, spread

    with jax.named_scope("stats1"):
        innovation, spread = stats(1)
        squares = jnp.sum(innovation * innovation, axis=1, keepdims=True)
        widths = jnp.sum(spread + small[1, 2:3, :], axis=1, keepdims=True)
        line = lax.broadcasted_iota(jnp.int32, (8, 128), 0)
        slots[r] = jnp.where(line < 4, squares, widths)

    def tell(o, c):
        remote(slots.at[r], slots.at[r], i_send, i_recv, region=lax.rem(r + o, regions)).start()
        return c

    lax.fori_loop(1, regions, tell, 0)
    told = slots.at[pl.ds(0, regions - 1)]
    tells = remote(told, told, i_send, i_recv, region=after)

    def gain_of(l, slot):
        with jax.named_scope("take"):
            take_own(l).wait()
            for copy in e_copies(l):
                copy.wait_recv()
        state = recv[l].astype(F32)
        mean = jnp.sum(state, axis=0, keepdims=True) / MEMBERS
        anom = (state - mean).astype(BF16)
        means[slot, 0:1, :] = mean
        anoms[slot] = anom
        for w in range(3):
            at = pl.ds(w * n_obs, n_obs)
            gain[slot, at, :] = (dot(anom_t[at, :], anom) * taper[at, :]).astype(BF16)

    with jax.named_scope("beside1"):
        for copy in from_beside(1):
            copy.wait_recv()
    with jax.named_scope("stats02"):
        stats(0)
        stats(2)
    with jax.named_scope("gain0"):
        gain_of(0, 0)
    with jax.named_scope("beside0"):
        for copy in from_beside(0):
            copy.wait_recv()
    with jax.named_scope("infl"):
        tells.wait_recv()
    total = jnp.sum(slots[...], axis=0)
    infl = total[0:1, 0:1] / total[4:5, 0:1]
    root = jnp.sqrt(infl)
    infl_ref[0, 0] = infl[0, 0]

    with jax.named_scope("pert"):
        for w in range(3):
            mean, spread = tot[w, 0:1, :], tot[w, 1:2, :]
            factor = infl / (infl * spread + small[w, 2:3, :])
            innovation = small[w, 1:2, :] - mean
            dev = obs[w, 1].astype(F32) - mean
            moved = innovation + obs[w, 0].astype(F32) - root * dev
            pert[:, pl.ds(w * n_obs, n_obs)] = (moved * factor).astype(BF16)

    def b_copies(l):
        return [
            remote(back.at[l, rows(p), :], out.at[l, :, cols(j)], b_send.at[k], b_recv.at[k, l], member=p)
            for k, p in enumerate(others)
        ]

    def analyse(l, c):
        slot = lax.rem(l, 2)
        with jax.named_scope("inc"):
            increment = dot(pert[...], gain[slot])
            back[l] = (means[slot, 0:1, :] + root * anoms[slot].astype(F32) + increment).astype(BF16)
        for copy in b_copies(l):
            copy.start()
        out[l, :, cols(j)] = back[l, rows(j), :]

        @pl.when(l < n_var - 1)
        def _():
            with jax.named_scope("gain"):
                gain_of(l + 1, 1 - slot)

        return c

    lax.fori_loop(0, n_var, analyse, 0)

    def finish(l, c):
        with jax.named_scope("fin"):
            for copy in b_copies(l):
                copy.wait_recv()
        return c

    lax.fori_loop(0, n_var, finish, 0)

    with jax.named_scope("sent"):
        whole = recv.at[:, pl.ds(0, own), :]
        for sems in (e_send, b_send):
            for k, p in enumerate(others):
                remote(whole, whole, sems.at[k], e_recv.at[0, 0], member=p).wait_send()
        for q in range(2):
            for copy in o_copies(q):
                copy.wait_send()
            for copy in from_beside(q):
                copy.wait_send()
        from_depth.wait_send()
        for copy in small_copies:
            copy.wait_send()
        swap.wait_send()
        tells.wait_send()


def solution(mesh):
    regions, peers = mesh.shape["region"], mesh.shape["member"]

    def shards(ensemble, obs_weights, obs_tiles, obs_values, obs_error, obs_noise):
        n_var, own, n_tile = ensemble.shape
        n_obs = obs_tiles.shape[0]
        share, members = n_tile // peers, own * peers
        DMA = pltpu.SemaphoreType.DMA
        scratch = [
            pltpu.VMEM((n_var, own, n_tile), BF16),
            pltpu.SMEM((n_var,), F32),
            pltpu.VMEM((1, n_obs), jnp.int32),
            pltpu.VMEM((3, 8, n_obs), F32),
            pltpu.VMEM((own, n_obs), F32),
            pltpu.VMEM((own, n_tile), BF16),
            pltpu.VMEM((n_tile, n_obs), BF16),
            pltpu.VMEM((2, own, n_obs), BF16),
            pltpu.VMEM((3, 2, members, n_obs), BF16),
            pltpu.VMEM((regions, 8, 128), F32),
            pltpu.VMEM((n_var, members, share), BF16),
            pltpu.VMEM((n_var, members, share), BF16),
            pltpu.VMEM((2, members, share), BF16),
            pltpu.VMEM((2, 8, share), F32),
            pltpu.VMEM((3 * n_obs, members), BF16),
            pltpu.VMEM((3 * n_obs, share), F32),
            pltpu.VMEM((2, 3 * n_obs, share), BF16),
            pltpu.VMEM((members, 3 * n_obs), BF16),
            pltpu.VMEM((3, 8, n_obs), F32),
            DMA((6,)),
            DMA((3,)),
            DMA((3, n_var)),
            DMA((3,)),
            DMA((3, n_var)),
            DMA((2, 3)),
            DMA((2, 3)),
            DMA,
            DMA,
            DMA((2, 2)),
            DMA((2, 2)),
            DMA((2,)),
            DMA((2,)),
            DMA,
            DMA,
            DMA,
            DMA,
            DMA((n_var,)),
        ]
        hbm = pl.BlockSpec(memory_space=pltpu.HBM)
        analysis, inflation = pl.pallas_call(
            lambda *refs: kernel(regions, peers, *refs),
            out_shape=(
                pltpu.VMEM(ensemble.shape, BF16),
                jax.ShapeDtypeStruct((1, 1), F32),
            ),
            in_specs=[hbm] * 6,
            out_specs=(pl.BlockSpec(memory_space=pltpu.VMEM), pl.BlockSpec(memory_space=pltpu.SMEM)),
            scratch_shapes=scratch,
            compiler_params=pltpu.CompilerParams(
                collective_id=0, has_side_effects=True, vmem_limit_bytes=56 * 2**20
            ),
        )(
            ensemble,
            obs_weights,
            obs_tiles.reshape(1, n_obs),
            obs_values.reshape(1, n_obs),
            obs_error.reshape(1, n_obs),
            obs_noise,
        )
        return analysis, inflation.reshape(())

    return jax.shard_map(
        shards,
        mesh=mesh,
        in_specs=(
            P("depth", "member", "region"),
            P("depth"),
            P("region"),
            P("region"),
            P("region"),
            P("member", "region"),
        ),
        out_specs=(P("depth", "member", "region"), P()),
        check_vma=False,
    )
```

time: 58.5 us -> 52.7 us (0.901)
  the two profiles are of different devices: /device:TPU:2 before, /device:TPU:1 now
where the time goes in v2:
time: 52.7 us; the launch traced here: 52.3 us
  Pallas kernels  48.9 us (93%)
  between operations  2.33 us (4%)
  local copies, waits for them, and re-layouts  1.08 us (2%)
    pallas_call x1, Pallas kernels, shards(): pl.pallas_call(lambda *refs: kernel(regions, peers, *refs), out_shape=(pl...  48.9 us
    unnamed x1, local copies, waits for them, and re-layouts  1.08 us

profile of v2, /device:TPU:1, one launch (start us, length us, event | category | flops | bytes accessed | tf_op | source)
XLA Modules:
  0.0 52.3 jit_solution(16609810974598477051)
XLA Ops:
  0.6 48.9 %shard_map.77 = (bf16[7,96,1024]{2,1,0:T(8,128)(2,1)S(1)}, f32[1,1]{1,0:T(1,128)}) custom-call(bf16[7,96,1024]{2,1,0:T(8,128)(2,1)} %refs_0_.1, f32[7]{0:T(128)} %refs_1_.1, s32[1,512]{1,0:T(1,128)} %bitcast.4, f32[1,512]{1,0:T(1,128)} %bitcast.5, f32[1,512]{1,0:T(1,128)} %bitcast.6, f32[96,512]{1,0:T(8,128)} %refs_5_.1), custom_call_target="tpu_custom_call" | custom-call | tf_op jit(solution)/shard_map/pallas_call | solution.py:405
  49.5 1.1 %copy.10 = bf16[7,96,1024]{2,1,0:T(8,128)(2,1)} copy(bf16[7,96,1024]{2,1,0:T(8,128)(2,1)S(1)} %get-tuple-element.6) | data formatting | bytes 2752512

commit v3 on v2

--- a/solution.py
+++ b/solution.py
@@ -7,6 +7,7 @@
 
 MEMBERS = 384
 RADIUS = 1024.0
+EARLY = 2
 MESH = pl.DeviceIdType.MESH
 F32 = jnp.float32
 BF16 = jnp.bfloat16
@@ -36,6 +37,7 @@
     hot,
     part,
     obs,
+    sums,
     slots,
     recv,
     back,
@@ -61,6 +63,8 @@
     s_recv,
     d_send,
     d_recv,
+    m_send,
+    m_recv,
     i_send,
     i_recv,
     own_sem,
@@ -73,7 +77,12 @@
     j = lax.axis_index("member")
     right, left, opp = lax.rem(j + 1, peers), lax.rem(j + 3, peers), lax.rem(j + 2, peers)
     after, before = lax.rem(r + 1, regions), lax.rem(r + regions - 1, regions)
-    others = (opp, right, left)
+    others = (right, left, opp)
+    sides = (
+        (0, after, r < regions - 1, r == regions // 2 - 1),
+        (1, before, r > 0, r == regions // 2),
+    )
+    near = 2 * lax.rem(r + 1, 2)
 
     def rows(b):
         return pl.ds(pl.multiple_of(b * own, 16), own)
@@ -100,6 +109,13 @@
     for p in others:
         greet(member=p)
     greet(depth=1 - d)
+    for k, p, has, seam in sides:
+
+        @pl.when(seam)
+        def _():
+            greet(region=p, depth=1 - d)
+
+    at_seam = jnp.logical_or(sides[0][3], sides[1][3]).astype(jnp.int32)
 
     loads = [
         pltpu.make_async_copy(ens_hbm, ens, load_sem.at[0]),
@@ -149,7 +165,7 @@
     with jax.named_scope("pick"):
         part[0] = dot(blend[...], hot[...]).astype(BF16)
     with jax.named_scope("barrier"):
-        pl.semaphore_wait(barrier, regions + 3)
+        pl.semaphore_wait(barrier, regions + 3 + at_seam)
 
     def e_copies(l):
         return [
@@ -166,45 +182,78 @@
         lax.fori_loop(first, last, body, 0)
 
     def o_copies(q):
-        block = obs.at[1, 1, rows(j), :] if q else obs.at[1, 0, rows(j), half(d)]
+        block = obs.at[1, q, rows(j), half(d)]
         return [
             remote(block, block, o_send.at[q, k], o_recv.at[q, k], member=p) for k, p in enumerate(others)
         ]
 
+    def to_depth(q, b):
+        block = obs.at[1, q, rows(b), half(d)]
+        remote(block, block, y_send.at[q], y_recv.at[q], depth=1 - d).start()
+
+    def from_depth(q):
+        three = obs.at[1, q, pl.ds(0, 3 * own), half(d)]
+        return remote(three, three, y_send.at[q], y_recv.at[q], depth=1 - d)
+
     def to_beside(q, b, h=None):
-        at = (rows(b), slice(None)) if h is None else (rows(b), half(h))
-        remote(obs.at[(1, q) + at], obs.at[(0, q) + at], n_send.at[q, 0], n_recv.at[q, 0], region=after).start()
-        remote(obs.at[(1, q) + at], obs.at[(2, q) + at], n_send.at[q, 1], n_recv.at[q, 1], region=before).start()
-
-    def from_beside(q):
-        return (
-            remote(obs.at[1, q], obs.at[0, q], n_send.at[q, 0], n_recv.at[q, 0], region=after),
-            remote(obs.at[1, q], obs.at[2, q], n_send.at[q, 1], n_recv.at[q, 1], region=before),
-        )
-
-    def to_depth(b):
-        block = obs.at[1, 0, rows(b), half(d)]
-        remote(block, block, y_send, y_recv, depth=1 - d).start()
-
-    three = obs.at[1, 0, pl.ds(0, 3 * own), half(d)]
-    from_depth = remote(three, three, y_send, y_recv, depth=1 - d)
-    small_copies = (
-        remote(small.at[1], small.at[0], s_send.at[0], s_recv.at[0], region=after),
-        remote(small.at[1], small.at[2], s_send.at[1], s_recv.at[1], region=before),
-    )
+        for k, p, has, seam in sides:
+
+            def send(part, **where):
+                at = (rows(b), slice(None)) if part is None else (rows(b), half(part))
+                remote(
+                    obs.at[(1, q) + at], obs.at[(2 * k, q) + at], n_send.at[q, k], n_recv.at[q, k], region=p, **where
+                ).start()
+
+            @pl.when(jnp.logical_and(has, jnp.logical_not(seam)))
+            def _():
+                send(h)
+
+            if h is None or h is d:
+
+                @pl.when(seam)
+                def _():
+                    send(d)
+                    send(d, depth=1 - d)
+
+    def beside(q, w):
+        k = w // 2
+        return remote(obs.at[1, q], obs.at[w, q], n_send.at[q, k], n_recv.at[q, k], region=after)
+
+    def has_window(w):
+        return jnp.logical_and(r + w > 0, r + w < regions + 1)
+
+    def small_copy(k, p):
+        return remote(small.at[1], small.at[2 * k], s_send.at[k], s_recv.at[k], region=p)
+
     swap = remote(part.at[0], part.at[1], d_send, d_recv, depth=1 - d)
 
     swap.start()
+    for k, p, has, seam in sides:
+
+        @pl.when(has)
+        def _():
+            small_copy(k, p).start()
+
     for copy in o_copies(0):
         copy.start()
-    send_ens(0, 1)
-    for copy in small_copies:
-        copy.start()
+    send_ens(0, EARLY)
     to_beside(0, j)
 
     with jax.named_scope("small"):
-        for copy in small_copies:
-            copy.wait_recv()
+        for k, has in ((0, r > 0), (1, r < regions - 1)):
+
+            @pl.when(has)
+            def _():
+                small_copy(k, after).wait_recv()
+
+            @pl.when(jnp.logical_not(has))
+            def _():
+                small[2 * k] = jnp.ones_like(small[1])
+                at = pl.ds(2 * k * n_obs, n_obs)
+                anom_t[at, :] = jnp.zeros((n_obs, MEMBERS), BF16)
+                gain[0, at, :] = jnp.zeros((n_obs, share), BF16)
+                pert[:, at] = jnp.zeros((MEMBERS, n_obs), BF16)
+
     lane = lax.broadcasted_iota(jnp.int32, (n_obs, 128), 1) + j * share
     shifts = (
         jnp.where(r == 0, -16.0 * RADIUS, -RADIUS),
@@ -215,46 +264,49 @@
         for w in range(3):
             spot = jnp.broadcast_to(small[w, 0:1, :] + shifts[w], (128, n_obs)).T
             for c in range(share // 128):
-                near = jnp.maximum(0.0, 1.0 - jnp.abs((lane + c * 128).astype(F32) - spot) / RADIUS)
-                taper[pl.ds(w * n_obs, n_obs), pl.ds(c * 128, 128)] = near * near / (MEMBERS - 1)
+                level = jnp.maximum(0.0, 1.0 - jnp.abs((lane + c * 128).astype(F32) - spot) / RADIUS)
+                taper[pl.ds(w * n_obs, n_obs), pl.ds(c * 128, 128)] = level * level / (MEMBERS - 1)
 
     with jax.named_scope("swap"):
         swap.wait_recv()
-    obs[1, 1, rows(j), :] = (part[0].astype(F32) + part[1].astype(F32)).astype(BF16)
-    for copy in o_copies(1):
+    mixed = (part[0].astype(F32) + part[1].astype(F32)).astype(BF16)
+    obs[1, 1, rows(j), :] = mixed
+    mixed = mixed.astype(F32)
+    part_sum = jnp.sum(mixed, axis=0, keepdims=True)
+    apart = mixed - part_sum / own
+    sums[j, 0:1, :] = part_sum
+    sums[j, 1:2, :] = jnp.sum(apart * apart, axis=0, keepdims=True)
+    m_copies = [
+        remote(sums.at[j], sums.at[j], m_send.at[k], m_recv.at[k], member=p) for k, p in enumerate(others)
+    ]
+    for copy in m_copies + o_copies(1):
         copy.start()
     to_beside(1, j)
-    send_ens(1, n_var)
+    send_ens(EARLY, n_var)
     with jax.named_scope("noise_x"):
-        for copy, b in zip(o_copies(0), (opp, left, right)):
+        for copy, b in zip(o_copies(0), (left, right, opp)):
             copy.wait_recv()
-            to_depth(b)
+            to_depth(0, b)
             to_beside(0, b, d)
-    with jax.named_scope("noise_y"):
-        from_depth.wait_recv()
-    for b in others:
-        to_beside(0, b, 1 - d)
-    with jax.named_scope("pred_x"):
-        for k, b in ((2, right), (1, left), (0, opp)):
-            o_copies(1)[k].wait_recv()
-            to_beside(1, b)
-
-    def stats(w):
-        pred = obs[w, 1].astype(F32)
-        mean = jnp.sum(pred, axis=0, keepdims=True) / MEMBERS
-        dev = pred - mean
-        spread = jnp.sum(dev * dev, axis=0, keepdims=True) / (MEMBERS - 1)
-        tot[w, 0:1, :] = mean
-        tot[w, 1:2, :] = spread
-        anom_t[pl.ds(w * n_obs, n_obs), :] = dev.T.astype(BF16)
-        return small[w, 1:2, :] - mean, spread
-
-    with jax.named_scope("stats1"):
-        innovation, spread = stats(1)
-        squares = jnp.sum(innovation * innovation, axis=1, keepdims=True)
-        widths = jnp.sum(spread + small[1, 2:3, :], axis=1, keepdims=True)
-        line = lax.broadcasted_iota(jnp.int32, (8, 128), 0)
-        slots[r] = jnp.where(line < 4, squares, widths)
+
+    with jax.named_scope("sums"):
+        for copy in m_copies:
+            copy.wait_recv()
+    mean = (sums[0, 0:1, :] + sums[1, 0:1, :] + sums[2, 0:1, :] + sums[3, 0:1, :]) / MEMBERS
+    squares = jnp.zeros_like(mean)
+    for p in range(peers):
+        off = sums[p, 0:1, :] / own - mean
+        squares = squares + (sums[p, 1:2, :] + own * off * off)
+    spread = squares / (MEMBERS - 1)
+    tot[1, 0:1, :] = mean
+    tot[1, 1:2, :] = spread
+    innovation = small[1, 1:2, :] - mean
+    line = lax.broadcasted_iota(jnp.int32, (8, 128), 0)
+    slots[r] = jnp.where(
+        line < 4,
+        jnp.sum(innovation * innovation, axis=1, keepdims=True),
+        jnp.sum(spread + small[1, 2:3, :], axis=1, keepdims=True),
+    )
 
     def tell(o, c):
         remote(slots.at[r], slots.at[r], i_send, i_recv, region=lax.rem(r + o, regions)).start()
@@ -264,46 +316,89 @@
     told = slots.at[pl.ds(0, regions - 1)]
     tells = remote(told, told, i_send, i_recv, region=after)
 
-    def gain_of(l, slot):
+    with jax.named_scope("pred_x"):
+        for copy, b in zip(o_copies(1), (left, right, opp)):
+            copy.wait_recv()
+            to_depth(1, b)
+            to_beside(1, b, d)
+    with jax.named_scope("noise_y"):
+        from_depth(0).wait_recv()
+    for b in others:
+        to_beside(0, b, 1 - d)
+    def window(w):
+        return pl.ds(pl.multiple_of(w * n_obs, n_obs), n_obs)
+
+    def turned(w, mean):
+        dev = obs[w, 1].astype(F32) - mean
+        anom_t[window(w), :] = dev.T.astype(BF16)
+        return dev
+
+    def stats(w):
+        mean = jnp.sum(obs[w, 1].astype(F32), axis=0, keepdims=True) / MEMBERS
+        dev = turned(w, mean)
+        tot[w, 0:1, :] = mean
+        tot[w, 1:2, :] = jnp.sum(dev * dev, axis=0, keepdims=True) / (MEMBERS - 1)
+
+    def anomalies_of(l, slot):
         with jax.named_scope("take"):
             take_own(l).wait()
             for copy in e_copies(l):
                 copy.wait_recv()
         state = recv[l].astype(F32)
         mean = jnp.sum(state, axis=0, keepdims=True) / MEMBERS
-        anom = (state - mean).astype(BF16)
         means[slot, 0:1, :] = mean
-        anoms[slot] = anom
-        for w in range(3):
-            at = pl.ds(w * n_obs, n_obs)
-            gain[slot, at, :] = (dot(anom_t[at, :], anom) * taper[at, :]).astype(BF16)
-
-    with jax.named_scope("beside1"):
-        for copy in from_beside(1):
-            copy.wait_recv()
-    with jax.named_scope("stats02"):
-        stats(0)
-        stats(2)
+        anoms[slot] = (state - mean).astype(BF16)
+
+    def gain_of(slot, w):
+        at = window(w)
+        gain[slot, at, :] = (dot(anom_t[at, :], anoms[slot]) * taper[at, :]).astype(BF16)
+
+    def perturbed(w, infl, root):
+        mean, spread = tot[w, 0:1, :], tot[w, 1:2, :]
+        factor = infl / (infl * spread + small[w, 2:3, :])
+        innovation = small[w, 1:2, :] - mean
+        dev = obs[w, 1].astype(F32) - mean
+        moved = innovation + obs[w, 0].astype(F32) - root * dev
+        pert[:, window(w)] = (moved * factor).astype(BF16)
+
+    with jax.named_scope("anom0"):
+        anomalies_of(0, 0)
+    with jax.named_scope("pred_y"):
+        from_depth(1).wait_recv()
+    for b in others:
+        to_beside(1, b, 1 - d)
     with jax.named_scope("gain0"):
-        gain_of(0, 0)
-    with jax.named_scope("beside0"):
-        for copy in from_beside(0):
-            copy.wait_recv()
+        turned(1, tot[1, 0:1, :])
+        gain_of(0, 1)
     with jax.named_scope("infl"):
         tells.wait_recv()
     total = jnp.sum(slots[...], axis=0)
     infl = total[0:1, 0:1] / total[4:5, 0:1]
     root = jnp.sqrt(infl)
-    infl_ref[0, 0] = infl[0, 0]
-
-    with jax.named_scope("pert"):
-        for w in range(3):
-            mean, spread = tot[w, 0:1, :], tot[w, 1:2, :]
-            factor = infl / (infl * spread + small[w, 2:3, :])
-            innovation = small[w, 1:2, :] - mean
-            dev = obs[w, 1].astype(F32) - mean
-            moved = innovation + obs[w, 0].astype(F32) - root * dev
-            pert[:, pl.ds(w * n_obs, n_obs)] = (moved * factor).astype(BF16)
+    infl_ref[...] = infl
+    with jax.named_scope("pert1"):
+        perturbed(1, infl, root)
+    with jax.named_scope("near1"):
+        beside(1, near).wait_recv()
+    with jax.named_scope("gainn"):
+        stats(near)
+        gain_of(0, near)
+    with jax.named_scope("near0"):
+        beside(0, near).wait_recv()
+    with jax.named_scope("pertn"):
+        perturbed(near, infl, root)
+
+    @pl.when(has_window(2 - near))
+    def _():
+        with jax.named_scope("far1"):
+            beside(1, 2 - near).wait_recv()
+        with jax.named_scope("gainf"):
+            stats(2 - near)
+            gain_of(0, 2 - near)
+        with jax.named_scope("far0"):
+            beside(0, 2 - near).wait_recv()
+        with jax.named_scope("pertf"):
+            perturbed(2 - near, infl, root)
 
     def b_copies(l):
         return [
@@ -323,7 +418,9 @@
         @pl.when(l < n_var - 1)
         def _():
             with jax.named_scope("gain"):
-                gain_of(l + 1, 1 - slot)
+                anomalies_of(l + 1, 1 - slot)
+                for w in range(3):
+                    gain_of(1 - slot, w)
 
         return c
 
@@ -345,10 +442,16 @@
         for q in range(2):
             for copy in o_copies(q):
                 copy.wait_send()
-            for copy in from_beside(q):
-                copy.wait_send()
-        from_depth.wait_send()
-        for copy in small_copies:
+            from_depth(q).wait_send()
+        for k, p, has, seam in sides:
+
+            @pl.when(has)
+            def _():
+                small_copy(k, after).wait_send()
+                for q in range(2):
+                    beside(q, 2 * k).wait_send()
+
+        for copy in m_copies:
             copy.wait_send()
         swap.wait_send()
         tells.wait_send()
@@ -372,6 +475,7 @@
             pltpu.VMEM((n_tile, n_obs), BF16),
             pltpu.VMEM((2, own, n_obs), BF16),
             pltpu.VMEM((3, 2, members, n_obs), BF16),
+            pltpu.VMEM((peers, 8, n_obs), F32),
             pltpu.VMEM((regions, 8, 128), F32),
             pltpu.VMEM((n_var, members, share), BF16),
             pltpu.VMEM((n_var, members, share), BF16),
@@ -389,14 +493,16 @@
             DMA((3, n_var)),
             DMA((2, 3)),
             DMA((2, 3)),
-            DMA,
-            DMA,
+            DMA((2,)),
+            DMA((2,)),
             DMA((2, 2)),
             DMA((2, 2)),
             DMA((2,)),
             DMA((2,)),
             DMA,
             DMA,
+            DMA((3,)),
+            DMA((3,)),
             DMA,
             DMA,
             DMA((n_var,)),
@@ -406,10 +512,10 @@
             lambda *refs: kernel(regions, peers, *refs),
             out_shape=(
                 pltpu.VMEM(ensemble.shape, BF16),
-                jax.ShapeDtypeStruct((1, 1), F32),
+                pltpu.VMEM((1, 1), F32),
             ),
             in_specs=[hbm] * 6,
-            out_specs=(pl.BlockSpec(memory_space=pltpu.VMEM), pl.BlockSpec(memory_space=pltpu.SMEM)),
+            out_specs=(pl.BlockSpec(memory_space=pltpu.VMEM), pl.BlockSpec(memory_space=pltpu.VMEM)),
             scratch_shapes=scratch,
             compiler_params=pltpu.CompilerParams(
                 collective_id=0, has_side_effects=True, vmem_limit_bytes=56 * 2**20

time: 52.7 us -> 48.8 us (0.926)
  Pallas kernels: 48.9 us -> 45.8 us
  between operations: 2.33 us -> 1.8 us
    pallas_call x1, Pallas kernels: 48.9 us -> 45.8 us  [shards(): pl.pallas_call(lambda *refs: kernel(regions, peers, *refs), out_shape=(pl...]
where the time goes in v3:
time: 48.8 us; the launch traced here: 48.7 us
  Pallas kernels  45.8 us (94%)
  between operations  1.8 us (4%)
  local copies, waits for them, and re-layouts  1.08 us (2%)
    pallas_call x1, Pallas kernels, shards(): pl.pallas_call(lambda *refs: kernel(regions, peers, *refs), out_shape=(pl...  45.8 us
    unnamed x1, local copies, waits for them, and re-layouts  1.08 us

profile of v3, /device:TPU:1, one launch (start us, length us, event | category | flops | bytes accessed | tf_op | source)
XLA Modules:
  0.0 48.7 jit_solution(9685835168043369761)
XLA Ops:
  0.6 45.8 %shard_map.77 = (bf16[7,96,1024]{2,1,0:T(8,128)(2,1)S(1)}, f32[1,1]{1,0:T(1,128)S(1)}) custom-call(bf16[7,96,1024]{2,1,0:T(8,128)(2,1)} %refs_0_.1, f32[7]{0:T(128)} %refs_1_.1, s32[1,512]{1,0:T(1,128)} %bitcast.4, f32[1,512]{1,0:T(1,128)} %bitcast.5, f32[1,512]{1,0:T(1,128)} %bitcast.6, f32[96,512]{1,0:T(8,128)} %refs_5_.1), custom_call_target="tpu_custom_call" | custom-call | tf_op jit(solution)/shard_map/pallas_call | solution.py:511
  46.5 1.1 %copy.10 = bf16[7,96,1024]{2,1,0:T(8,128)(2,1)} copy(bf16[7,96,1024]{2,1,0:T(8,128)(2,1)S(1)} %get-tuple-element.6) | data formatting | bytes 2752512

commit v4 on v3

--- a/solution.py
+++ b/solution.py
@@ -7,7 +7,8 @@
 
 MEMBERS = 384
 RADIUS = 1024.0
-EARLY = 2
+RING = 4
+EARLY = 1
 MESH = pl.DeviceIdType.MESH
 F32 = jnp.float32
 BF16 = jnp.bfloat16
@@ -20,6 +21,7 @@
 def kernel(
     regions,
     peers,
+    ring,
     ens_hbm,
     wts_hbm,
     tiles_hbm,
@@ -78,6 +80,10 @@
     right, left, opp = lax.rem(j + 1, peers), lax.rem(j + 3, peers), lax.rem(j + 2, peers)
     after, before = lax.rem(r + 1, regions), lax.rem(r + regions - 1, regions)
     others = (right, left, opp)
+    core, z, y = lax.rem(r, 2), lax.rem(r // 2, ring), r // (2 * ring)
+    ring_peers = [r - 2 * z + 2 * lax.rem(z + o, ring) for o in range(1, ring)]
+    across = r + 2 * ring * (1 - 2 * y)
+    other_core = 1 - 2 * core
     sides = (
         (0, after, r < regions - 1, r == regions // 2 - 1),
         (1, before, r > 0, r == regions // 2),
@@ -101,21 +107,24 @@
     def greet(**where):
         pl.semaphore_signal(barrier, inc=1, device_id=where, device_id_type=MESH)
 
-    def greet_region(o, c):
-        greet(region=lax.rem(r + o, regions))
-        return c
-
-    lax.fori_loop(1, regions, greet_region, 0)
     for p in others:
         greet(member=p)
+    for p in ring_peers + [across, across + other_core]:
+        greet(region=p)
     greet(depth=1 - d)
     for k, p, has, seam in sides:
+
+        @pl.when(has)
+        def _():
+            greet(region=p)
 
         @pl.when(seam)
         def _():
             greet(region=p, depth=1 - d)
 
-    at_seam = jnp.logical_or(sides[0][3], sides[1][3]).astype(jnp.int32)
+    greeted = ring + 5
+    for k, p, has, seam in sides:
+        greeted = greeted + has.astype(jnp.int32) + seam.astype(jnp.int32)
 
     loads = [
         pltpu.make_async_copy(ens_hbm, ens, load_sem.at[0]),
@@ -129,7 +138,7 @@
         copy.start()
 
     def take_own(l):
-        return pltpu.make_async_copy(ens_hbm.at[l, :, cols(j)], recv.at[l, rows(j), :], own_sem.at[l])
+        return pltpu.make_async_copy(ens_hbm.at[l, :, cols(j)], recv.at[l, rows(j), :], own_sem)
 
     lax.fori_loop(0, n_var, lambda l, c: (take_own(l).start(), c)[1], 0)
 
@@ -159,18 +168,15 @@
         for copy in loads[3:]:
             copy.wait()
         obs[1, 0, rows(j), :] = (jnp.sqrt(small[1, 2:3, :]) * noise[...]).astype(BF16)
-    with jax.named_scope("blend"):
+    with jax.named_scope("ens"):
         loads[0].wait()
-        lax.fori_loop(0, own // 16, blended, 0)
-    with jax.named_scope("pick"):
-        part[0] = dot(blend[...], hot[...]).astype(BF16)
     with jax.named_scope("barrier"):
-        pl.semaphore_wait(barrier, regions + 3 + at_seam)
+        pl.semaphore_wait(barrier, greeted)
 
     def e_copies(l):
         return [
-            remote(ens.at[l, :, cols(p)], recv.at[l, rows(j), :], e_send.at[k], e_recv.at[k, l], member=p)
-            for k, p in enumerate(others)
+            remote(ens.at[l, :, cols(p)], recv.at[l, rows(j), :], e_send, e_recv.at[l], member=p)
+            for p in others
         ]
 
     def send_ens(first, last):
@@ -184,16 +190,24 @@
     def o_copies(q):
         block = obs.at[1, q, rows(j), half(d)]
         return [
-            remote(block, block, o_send.at[q, k], o_recv.at[q, k], member=p) for k, p in enumerate(others)
+            remote(block, block, o_send, o_recv.at[q * (1 + k)], member=p) for k, p in enumerate(others)
         ]
 
-    def to_depth(q, b):
-        block = obs.at[1, q, rows(b), half(d)]
-        remote(block, block, y_send.at[q], y_recv.at[q], depth=1 - d).start()
+    def over_depth(q, k, h):
+        block = obs.at[1, q, rows((left, right, opp)[k]), half(h)]
+        return remote(block, block, y_send, y_recv.at[q * (1 + k)], depth=1 - d)
+
+    def to_depth(q, k):
+        over_depth(q, k, d).start()
 
     def from_depth(q):
-        three = obs.at[1, q, pl.ds(0, 3 * own), half(d)]
-        return remote(three, three, y_send.at[q], y_recv.at[q], depth=1 - d)
+        if not q:
+            three = obs.at[1, 0, pl.ds(0, 3 * own), half(1 - d)]
+            remote(three, three, y_send, y_recv.at[0], depth=1 - d).wait_recv()
+        for k, b in enumerate((left, right, opp)):
+            if q:
+                over_depth(q, k, 1 - d).wait_recv()
+            to_beside(q, b, 1 - d)
 
     def to_beside(q, b, h=None):
         for k, p, has, seam in sides:
@@ -201,7 +215,7 @@
             def send(part, **where):
                 at = (rows(b), slice(None)) if part is None else (rows(b), half(part))
                 remote(
-                    obs.at[(1, q) + at], obs.at[(2 * k, q) + at], n_send.at[q, k], n_recv.at[q, k], region=p, **where
+                    obs.at[(1, q) + at], obs.at[(2 * k, q) + at], n_send.at[k], n_recv.at[q, k], region=p, **where
                 ).start()
 
             @pl.when(jnp.logical_and(has, jnp.logical_not(seam)))
@@ -215,9 +229,19 @@
                     send(d)
                     send(d, depth=1 - d)
 
+    def take_half(q):
+        if not q:
+            three = obs.at[1, 0, pl.ds(0, 3 * own), half(d)]
+            remote(three, three, o_send, o_recv.at[0], member=opp).wait_recv()
+        for k, b in enumerate((left, right, opp)):
+            if q:
+                o_copies(q)[k].wait_recv()
+            to_depth(q, k)
+            to_beside(q, b, d)
+
     def beside(q, w):
         k = w // 2
-        return remote(obs.at[1, q], obs.at[w, q], n_send.at[q, k], n_recv.at[q, k], region=after)
+        return remote(obs.at[1, q], obs.at[w, q], n_send.at[k], n_recv.at[q, k], region=after)
 
     def has_window(w):
         return jnp.logical_and(r + w > 0, r + w < regions + 1)
@@ -227,6 +251,13 @@
 
     swap = remote(part.at[0], part.at[1], d_send, d_recv, depth=1 - d)
 
+    for copy in o_copies(0):
+        copy.start()
+    send_ens(0, EARLY)
+    with jax.named_scope("blend"):
+        lax.fori_loop(0, own // 16, blended, 0)
+    with jax.named_scope("pick"):
+        part[0] = dot(blend[...], hot[...]).astype(BF16)
     swap.start()
     for k, p, has, seam in sides:
 
@@ -234,9 +265,6 @@
         def _():
             small_copy(k, p).start()
 
-    for copy in o_copies(0):
-        copy.start()
-    send_ens(0, EARLY)
     to_beside(0, j)
 
     with jax.named_scope("small"):
@@ -277,21 +305,19 @@
     sums[j, 0:1, :] = part_sum
     sums[j, 1:2, :] = jnp.sum(apart * apart, axis=0, keepdims=True)
     m_copies = [
-        remote(sums.at[j], sums.at[j], m_send.at[k], m_recv.at[k], member=p) for k, p in enumerate(others)
+        remote(sums.at[j], sums.at[j], m_send, m_recv, member=p) for p in others
     ]
     for copy in m_copies + o_copies(1):
         copy.start()
     to_beside(1, j)
     send_ens(EARLY, n_var)
     with jax.named_scope("noise_x"):
-        for copy, b in zip(o_copies(0), (left, right, opp)):
-            copy.wait_recv()
-            to_depth(0, b)
-            to_beside(0, b, d)
+        take_half(0)
 
     with jax.named_scope("sums"):
-        for copy in m_copies:
-            copy.wait_recv()
+        three_sums = sums.at[pl.ds(0, 3)]
+        summed = remote(three_sums, three_sums, m_send, m_recv, member=opp)
+        summed.wait_recv()
     mean = (sums[0, 0:1, :] + sums[1, 0:1, :] + sums[2, 0:1, :] + sums[3, 0:1, :]) / MEMBERS
     squares = jnp.zeros_like(mean)
     for p in range(peers):
@@ -302,29 +328,29 @@
     tot[1, 1:2, :] = spread
     innovation = small[1, 1:2, :] - mean
     line = lax.broadcasted_iota(jnp.int32, (8, 128), 0)
-    slots[r] = jnp.where(
+    slots[0, z] = jnp.where(
         line < 4,
         jnp.sum(innovation * innovation, axis=1, keepdims=True),
         jnp.sum(spread + small[1, 2:3, :], axis=1, keepdims=True),
     )
 
-    def tell(o, c):
-        remote(slots.at[r], slots.at[r], i_send, i_recv, region=lax.rem(r + o, regions)).start()
-        return c
-
-    lax.fori_loop(1, regions, tell, 0)
-    told = slots.at[pl.ds(0, regions - 1)]
-    tells = remote(told, told, i_send, i_recv, region=after)
-
+    def tell(step, at, targets):
+        for p in targets:
+            remote(slots.at[step, at], slots.at[step, at], i_send.at[step], i_recv.at[step], region=p).start()
+
+    def told(step):
+        block = slots.at[step, pl.ds(0, 3)]
+        return remote(block, block, i_send.at[step], i_recv.at[step], region=after)
+
+    tell(0, z, ring_peers)
     with jax.named_scope("pred_x"):
-        for copy, b in zip(o_copies(1), (left, right, opp)):
-            copy.wait_recv()
-            to_depth(1, b)
-            to_beside(1, b, d)
+        take_half(1)
     with jax.named_scope("noise_y"):
-        from_depth(0).wait_recv()
-    for b in others:
-        to_beside(0, b, 1 - d)
+        from_depth(0)
+    with jax.named_scope("told"):
+        told(0).wait_recv()
+        slots[1, 2 * y + core] = jnp.sum(slots[0], axis=0)
+        tell(1, 2 * y + core, (r + other_core, across, across + other_core))
     def window(w):
         return pl.ds(pl.multiple_of(w * n_obs, n_obs), n_obs)
 
@@ -341,9 +367,8 @@
 
     def anomalies_of(l, slot):
         with jax.named_scope("take"):
-            take_own(l).wait()
-            for copy in e_copies(l):
-                copy.wait_recv()
+            block = recv.at[l, pl.ds(0, 3 * own), :]
+            remote(block, block, e_send, e_recv.at[l], member=opp).wait_recv()
         state = recv[l].astype(F32)
         mean = jnp.sum(state, axis=0, keepdims=True) / MEMBERS
         means[slot, 0:1, :] = mean
@@ -362,17 +387,16 @@
         pert[:, window(w)] = (moved * factor).astype(BF16)
 
     with jax.named_scope("anom0"):
+        pltpu.make_async_copy(ens_hbm.at[:, :, cols(j)], recv.at[:, rows(j), :], own_sem).wait()
         anomalies_of(0, 0)
     with jax.named_scope("pred_y"):
-        from_depth(1).wait_recv()
-    for b in others:
-        to_beside(1, b, 1 - d)
+        from_depth(1)
     with jax.named_scope("gain0"):
         turned(1, tot[1, 0:1, :])
         gain_of(0, 1)
     with jax.named_scope("infl"):
-        tells.wait_recv()
-    total = jnp.sum(slots[...], axis=0)
+        told(1).wait_recv()
+    total = jnp.sum(slots[1], axis=0)
     infl = total[0:1, 0:1] / total[4:5, 0:1]
     root = jnp.sqrt(infl)
     infl_ref[...] = infl
@@ -402,7 +426,7 @@
 
     def b_copies(l):
         return [
-            remote(back.at[l, rows(p), :], out.at[l, :, cols(j)], b_send.at[k], b_recv.at[k, l], member=p)
+            remote(back.at[l, rows(p), :], out.at[l, :, cols(j)], b_send, b_recv, member=p)
             for k, p in enumerate(others)
         ]
 
@@ -426,35 +450,28 @@
 
     lax.fori_loop(0, n_var, analyse, 0)
 
-    def finish(l, c):
-        with jax.named_scope("fin"):
-            for copy in b_copies(l):
-                copy.wait_recv()
-        return c
-
-    lax.fori_loop(0, n_var, finish, 0)
+    with jax.named_scope("fin"):
+        back_in = back.at[:, pl.ds(0, 3 * own), :]
+        remote(back_in, back_in, b_send, b_recv, member=opp).wait_recv()
 
     with jax.named_scope("sent"):
-        whole = recv.at[:, pl.ds(0, own), :]
-        for sems in (e_send, b_send):
-            for k, p in enumerate(others):
-                remote(whole, whole, sems.at[k], e_recv.at[0, 0], member=p).wait_send()
-        for q in range(2):
-            for copy in o_copies(q):
-                copy.wait_send()
-            from_depth(q).wait_send()
+        remote(back_in, back_in, b_send, b_recv, member=opp).wait_send()
+        ens_in = recv.at[:, pl.ds(0, 3 * own), :]
+        remote(ens_in, ens_in, e_send, e_recv.at[0], member=opp).wait_send()
+        halves = obs.at[1, 0, pl.ds(0, 3 * own), :]
+        remote(halves, halves, o_send, o_recv.at[0], member=opp).wait_send()
+        remote(halves, halves, y_send, y_recv.at[0], depth=1 - d).wait_send()
         for k, p, has, seam in sides:
 
             @pl.when(has)
             def _():
                 small_copy(k, after).wait_send()
-                for q in range(2):
-                    beside(q, 2 * k).wait_send()
-
-        for copy in m_copies:
-            copy.wait_send()
+                remote(obs.at[1], obs.at[2 * k], n_send.at[k], n_recv.at[0, k], region=after).wait_send()
+
+        summed.wait_send()
         swap.wait_send()
-        tells.wait_send()
+        told(0).wait_send()
+        told(1).wait_send()
 
 
 def solution(mesh):
@@ -475,8 +492,8 @@
             pltpu.VMEM((n_tile, n_obs), BF16),
             pltpu.VMEM((2, own, n_obs), BF16),
             pltpu.VMEM((3, 2, members, n_obs), BF16),
-            pltpu.VMEM((peers, 8, n_obs), F32),
-            pltpu.VMEM((regions, 8, 128), F32),
+            pltpu.VMEM((peers, 2, n_obs), F32),
+            pltpu.VMEM((2, RING, 8, 128), F32),
             pltpu.VMEM((n_var, members, share), BF16),
             pltpu.VMEM((n_var, members, share), BF16),
             pltpu.VMEM((2, members, share), BF16),
@@ -487,29 +504,29 @@
             pltpu.VMEM((members, 3 * n_obs), BF16),
             pltpu.VMEM((3, 8, n_obs), F32),
             DMA((6,)),
-            DMA((3,)),
-            DMA((3, n_var)),
-            DMA((3,)),
-            DMA((3, n_var)),
-            DMA((2, 3)),
-            DMA((2, 3)),
+            DMA,
+            DMA((n_var,)),
+            DMA,
+            DMA,
+            DMA,
+            DMA((4,)),
+            DMA,
+            DMA((4,)),
             DMA((2,)),
-            DMA((2,)),
-            DMA((2, 2)),
             DMA((2, 2)),
             DMA((2,)),
             DMA((2,)),
             DMA,
             DMA,
-            DMA((3,)),
-            DMA((3,)),
-            DMA,
-            DMA,
-            DMA((n_var,)),
+            DMA,
+            DMA,
+            DMA((2,)),
+            DMA((2,)),
+            DMA,
         ]
         hbm = pl.BlockSpec(memory_space=pltpu.HBM)
         analysis, inflation = pl.pallas_call(
-            lambda *refs: kernel(regions, peers, *refs),
+            lambda *refs: kernel(regions, peers, RING, *refs),
             out_shape=(
                 pltpu.VMEM(ensemble.shape, BF16),
                 pltpu.VMEM((1, 1), F32),

time: 48.8 us -> 47.4 us (0.971)
  Pallas kernels: 45.8 us -> 44.4 us
    pallas_call x1, Pallas kernels: 45.8 us -> 44.4 us  [shards(): pl.pallas_call(lambda *refs: kernel(regions, peers, RING, *refs), out_sha...]
where the time goes in v4:
time: 47.4 us; the launch traced here: 47.2 us
  Pallas kernels  44.4 us (94%)
  between operations  1.8 us (4%)
  local copies, waits for them, and re-layouts  1.08 us (2%)
    pallas_call x1, Pallas kernels, shards(): pl.pallas_call(lambda *refs: kernel(regions, peers, RING, *refs), out_sha...  44.4 us
    unnamed x1, local copies, waits for them, and re-layouts  1.08 us

profile of v4, /device:TPU:1, one launch (start us, length us, event | category | flops | bytes accessed | tf_op | source)
XLA Modules:
  0.0 47.2 jit_solution(10436607836021428140)
XLA Ops:
  0.6 44.4 %shard_map.77 = (bf16[7,96,1024]{2,1,0:T(8,128)(2,1)S(1)}, f32[1,1]{1,0:T(1,128)S(1)}) custom-call(bf16[7,96,1024]{2,1,0:T(8,128)(2,1)} %refs_0_.1, f32[7]{0:T(128)} %refs_1_.1, s32[1,512]{1,0:T(1,128)} %bitcast.4, f32[1,512]{1,0:T(1,128)} %bitcast.5, f32[1,512]{1,0:T(1,128)} %bitcast.6, f32[96,512]{1,0:T(8,128)} %refs_5_.1), custom_call_target="tpu_custom_call" | custom-call | tf_op jit(solution)/shard_map/pallas_call | solution.py:528
  45.0 1.1 %copy.10 = bf16[7,96,1024]{2,1,0:T(8,128)(2,1)} copy(bf16[7,96,1024]{2,1,0:T(8,128)(2,1)S(1)} %get-tuple-element.6) | data formatting | bytes 2752512

commit v5 on v4

--- a/solution.py
+++ b/solution.py
@@ -79,7 +79,7 @@
     j = lax.axis_index("member")
     right, left, opp = lax.rem(j + 1, peers), lax.rem(j + 3, peers), lax.rem(j + 2, peers)
     after, before = lax.rem(r + 1, regions), lax.rem(r + regions - 1, regions)
-    others = (right, left, opp)
+    others = (opp, right, left)
     core, z, y = lax.rem(r, 2), lax.rem(r // 2, ring), r // (2 * ring)
     ring_peers = [r - 2 * z + 2 * lax.rem(z + o, ring) for o in range(1, ring)]
     across = r + 2 * ring * (1 - 2 * y)
@@ -194,7 +194,7 @@
         ]
 
     def over_depth(q, k, h):
-        block = obs.at[1, q, rows((left, right, opp)[k]), half(h)]
+        block = obs.at[1, q, rows((opp, left, right)[k]), half(h)]
         return remote(block, block, y_send, y_recv.at[q * (1 + k)], depth=1 - d)
 
     def to_depth(q, k):
@@ -204,7 +204,7 @@
         if not q:
             three = obs.at[1, 0, pl.ds(0, 3 * own), half(1 - d)]
             remote(three, three, y_send, y_recv.at[0], depth=1 - d).wait_recv()
-        for k, b in enumerate((left, right, opp)):
+        for k, b in enumerate((opp, left, right)):
             if q:
                 over_depth(q, k, 1 - d).wait_recv()
             to_beside(q, b, 1 - d)
@@ -233,7 +233,7 @@
         if not q:
             three = obs.at[1, 0, pl.ds(0, 3 * own), half(d)]
             remote(three, three, o_send, o_recv.at[0], member=opp).wait_recv()
-        for k, b in enumerate((left, right, opp)):
+        for k, b in enumerate((opp, left, right)):
             if q:
                 o_copies(q)[k].wait_recv()
             to_depth(q, k)
@@ -253,7 +253,9 @@
 
     for copy in o_copies(0):
         copy.start()
-    send_ens(0, EARLY)
+    send_ens(0, 1)
+    for copy in e_copies(1)[:EARLY]:
+        copy.start()
     with jax.named_scope("blend"):
         lax.fori_loop(0, own // 16, blended, 0)
     with jax.named_scope("pick"):
@@ -310,7 +312,9 @@
     for copy in m_copies + o_copies(1):
         copy.start()
     to_beside(1, j)
-    send_ens(EARLY, n_var)
+    for copy in e_copies(1)[EARLY:]:
+        copy.start()
+    send_ens(2, n_var)
     with jax.named_scope("noise_x"):
         take_half(0)
 
@@ -345,18 +349,23 @@
     tell(0, z, ring_peers)
     with jax.named_scope("pred_x"):
         take_half(1)
+
+    def tell_on():
+        with jax.named_scope("told"):
+            told(0).wait_recv()
+            slots[1, 2 * y + core] = jnp.sum(slots[0], axis=0)
+            tell(1, 2 * y + core, (r + other_core, across, across + other_core))
+
+    pl.when(z == ring - 1)(tell_on)
     with jax.named_scope("noise_y"):
         from_depth(0)
-    with jax.named_scope("told"):
-        told(0).wait_recv()
-        slots[1, 2 * y + core] = jnp.sum(slots[0], axis=0)
-        tell(1, 2 * y + core, (r + other_core, across, across + other_core))
+    pl.when(z < ring - 1)(tell_on)
     def window(w):
         return pl.ds(pl.multiple_of(w * n_obs, n_obs), n_obs)
 
     def turned(w, mean):
         dev = obs[w, 1].astype(F32) - mean
-        anom_t[window(w), :] = dev.T.astype(BF16)
+        anom_t[window(w), :] = dev.astype(BF16).T
         return dev
 
     def stats(w):
@@ -394,6 +403,21 @@
     with jax.named_scope("gain0"):
         turned(1, tot[1, 0:1, :])
         gain_of(0, 1)
+    with jax.named_scope("near1"):
+        beside(1, near).wait_recv()
+    with jax.named_scope("gainn"):
+        stats(near)
+        gain_of(0, near)
+
+    def far_gain():
+        with jax.named_scope("far1"):
+            beside(1, 2 - near).wait_recv()
+        with jax.named_scope("gainf"):
+            stats(2 - near)
+            gain_of(0, 2 - near)
+
+    has_far = has_window(2 - near)
+    pl.when(jnp.logical_and(has_far, core == 0))(far_gain)
     with jax.named_scope("infl"):
         told(1).wait_recv()
     total = jnp.sum(slots[1], axis=0)
@@ -402,23 +426,15 @@
     infl_ref[...] = infl
     with jax.named_scope("pert1"):
         perturbed(1, infl, root)
-    with jax.named_scope("near1"):
-        beside(1, near).wait_recv()
-    with jax.named_scope("gainn"):
-        stats(near)
-        gain_of(0, near)
     with jax.named_scope("near0"):
         beside(0, near).wait_recv()
     with jax.named_scope("pertn"):
         perturbed(near, infl, root)
 
-    @pl.when(has_window(2 - near))
+    pl.when(jnp.logical_and(has_far, core == 1))(far_gain)
+
+    @pl.when(has_far)
     def _():
-        with jax.named_scope("far1"):
-            beside(1, 2 - near).wait_recv()
-        with jax.named_scope("gainf"):
-            stats(2 - near)
-            gain_of(0, 2 - near)
         with jax.named_scope("far0"):
             beside(0, 2 - near).wait_recv()
         with jax.named_scope("pertf"):

time: 47.4 us -> 46.6 us (0.983)
  Pallas kernels: 44.4 us -> 43.2 us
    pallas_call x1, Pallas kernels: 44.4 us -> 43.2 us  [shards(): pl.pallas_call(lambda *refs: kernel(regions, peers, RING, *refs), out_sha...]
where the time goes in v5:
time: 46.6 us; the launch traced here: 46.1 us
  Pallas kernels  43.2 us (93%)
  between operations  1.8 us (4%)
  local copies, waits for them, and re-layouts  1.08 us (2%)
    pallas_call x1, Pallas kernels, shards(): pl.pallas_call(lambda *refs: kernel(regions, peers, RING, *refs), out_sha...  43.2 us
    unnamed x1, local copies, waits for them, and re-layouts  1.08 us

profile of v5, /device:TPU:1, one launch (start us, length us, event | category | flops | bytes accessed | tf_op | source)
XLA Modules:
  0.0 46.1 jit_solution(12445184694802595660)
XLA Ops:
  0.6 43.2 %shard_map.77 = (bf16[7,96,1024]{2,1,0:T(8,128)(2,1)S(1)}, f32[1,1]{1,0:T(1,128)S(1)}) custom-call(bf16[7,96,1024]{2,1,0:T(8,128)(2,1)} %refs_0_.1, f32[7]{0:T(128)} %refs_1_.1, s32[1,512]{1,0:T(1,128)} %bitcast.4, f32[1,512]{1,0:T(1,128)} %bitcast.5, f32[1,512]{1,0:T(1,128)} %bitcast.6, f32[96,512]{1,0:T(8,128)} %refs_5_.1), custom_call_target="tpu_custom_call" | custom-call | tf_op jit(solution)/shard_map/pallas_call | solution.py:544
  43.9 1.1 %copy.10 = bf16[7,96,1024]{2,1,0:T(8,128)(2,1)} copy(bf16[7,96,1024]{2,1,0:T(8,128)(2,1)S(1)} %get-tuple-element.6) | data formatting | bytes 2752512

commit v6 on v5

--- a/solution.py
+++ b/solution.py
@@ -8,6 +8,7 @@
 MEMBERS = 384
 RADIUS = 1024.0
 RING = 4
+CHUNK = 256
 EARLY = 1
 MESH = pl.DeviceIdType.MESH
 F32 = jnp.float32
@@ -35,8 +36,6 @@
     spots,
     small,
     noise,
-    blend,
-    hot,
     part,
     obs,
     sums,
@@ -69,7 +68,6 @@
     m_recv,
     i_send,
     i_recv,
-    own_sem,
 ):
     n_var, own, n_tile = ens.shape
     n_obs = noise.shape[1]
@@ -137,33 +135,6 @@
     for copy in loads:
         copy.start()
 
-    def take_own(l):
-        return pltpu.make_async_copy(ens_hbm.at[l, :, cols(j)], recv.at[l, rows(j), :], own_sem)
-
-    lax.fori_loop(0, n_var, lambda l, c: (take_own(l).start(), c)[1], 0)
-
-    def blended(i, c):
-        at = pl.ds(pl.multiple_of(i * 16, 16), 16)
-        total = wts[0] * ens[0, at, :].astype(F32)
-        for l in range(1, n_var):
-            total = total + wts[l] * ens[l, at, :].astype(F32)
-        blend[at, :] = total.astype(BF16)
-        return c
-
-    with jax.named_scope("load_small"):
-        loads[1].wait()
-        loads[2].wait()
-    tile_row = spots[...].astype(F32)
-    small[1, 0:1, :] = tile_row
-
-    def one_hot(i, c):
-        at = pl.ds(pl.multiple_of(i * 128, 128), 128)
-        index = (lax.broadcasted_iota(jnp.int32, (128, n_obs), 0) + i * 128).astype(F32)
-        hot[at, :] = jnp.where(index == tile_row, 1.0, 0.0).astype(BF16)
-        return c
-
-    with jax.named_scope("hot"):
-        lax.fori_loop(0, n_tile // 128, one_hot, 0)
     with jax.named_scope("noise"):
         for copy in loads[3:]:
             copy.wait()
@@ -186,6 +157,26 @@
             return c
 
         lax.fori_loop(first, last, body, 0)
+
+    last = n_var - 1
+
+    def last_copies():
+        to_right, to_left = dict(member=right), dict(member=left)
+        return [
+            remote(ens.at[last, :, cols(right)], recv.at[last, rows(j), :], e_send, e_recv.at[last + 2], **to_right),
+            remote(ens.at[last, :, cols(opp)], recv.at[last + 1, rows(j), :], e_send, e_recv.at[last + 3], **to_left),
+            remote(ens.at[last, :, cols(j)], recv.at[last + 1, rows(j), :], e_send, e_recv.at[last + 1], **to_right),
+            remote(ens.at[last, :, cols(left)], recv.at[last, rows(j), :], e_send, e_recv.at[last], **to_left),
+        ]
+
+    def pass_on():
+        first, second, _, _ = last_copies()
+        block = recv.at[last, rows(left), :]
+        first.wait_recv()
+        remote(block, recv.at[last + 1, rows(left), :], e_send, e_recv.at[last + 1], member=right).start()
+        block = recv.at[last + 1, rows(right), :]
+        second.wait_recv()
+        remote(block, recv.at[last, rows(right), :], e_send, e_recv.at[last], member=left).start()
 
     def o_copies(q):
         block = obs.at[1, q, rows(j), half(d)]
@@ -256,11 +247,25 @@
     send_ens(0, 1)
     for copy in e_copies(1)[:EARLY]:
         copy.start()
-    with jax.named_scope("blend"):
-        lax.fori_loop(0, own // 16, blended, 0)
+
+    with jax.named_scope("load_small"):
+        loads[1].wait()
+        loads[2].wait()
     with jax.named_scope("pick"):
-        part[0] = dot(blend[...], hot[...]).astype(BF16)
+        spot_row = spots[...]
+        picked = None
+        for c in range(n_tile // CHUNK):
+            at = pl.ds(c * CHUNK, CHUNK)
+            index = lax.broadcasted_iota(jnp.int32, (CHUNK, n_obs), 0) + c * CHUNK
+            hot = jnp.where(index == spot_row, 1.0, 0.0).astype(BF16)
+            blend = wts[0] * ens[0, :, at].astype(F32)
+            for l in range(1, n_var):
+                blend = blend + wts[l] * ens[l, :, at].astype(F32)
+            term = dot(blend.astype(BF16), hot)
+            picked = term if picked is None else picked + term
+        part[0] = picked.astype(BF16)
     swap.start()
+    small[1, 0:1, :] = spot_row.astype(F32)
     for k, p, has, seam in sides:
 
         @pl.when(has)
@@ -269,33 +274,12 @@
 
     to_beside(0, j)
 
-    with jax.named_scope("small"):
-        for k, has in ((0, r > 0), (1, r < regions - 1)):
-
-            @pl.when(has)
-            def _():
-                small_copy(k, after).wait_recv()
-
-            @pl.when(jnp.logical_not(has))
-            def _():
-                small[2 * k] = jnp.ones_like(small[1])
-                at = pl.ds(2 * k * n_obs, n_obs)
-                anom_t[at, :] = jnp.zeros((n_obs, MEMBERS), BF16)
-                gain[0, at, :] = jnp.zeros((n_obs, share), BF16)
-                pert[:, at] = jnp.zeros((MEMBERS, n_obs), BF16)
-
-    lane = lax.broadcasted_iota(jnp.int32, (n_obs, 128), 1) + j * share
-    shifts = (
-        jnp.where(r == 0, -16.0 * RADIUS, -RADIUS),
-        jnp.float32(0.0),
-        jnp.where(r == regions - 1, 16.0 * RADIUS, RADIUS),
-    )
-    with jax.named_scope("taper"):
-        for w in range(3):
-            spot = jnp.broadcast_to(small[w, 0:1, :] + shifts[w], (128, n_obs)).T
-            for c in range(share // 128):
-                level = jnp.maximum(0.0, 1.0 - jnp.abs((lane + c * 128).astype(F32) - spot) / RADIUS)
-                taper[pl.ds(w * n_obs, n_obs), pl.ds(c * 128, 128)] = level * level / (MEMBERS - 1)
+    def take_own(l, c):
+        recv[l, rows(j), :] = ens[l, :, cols(j)]
+        return c
+
+    lax.fori_loop(0, n_var, take_own, 0)
+    recv[last + 1, rows(j), :] = ens[last, :, cols(left)]
 
     with jax.named_scope("swap"):
         swap.wait_recv()
@@ -312,11 +296,43 @@
     for copy in m_copies + o_copies(1):
         copy.start()
     to_beside(1, j)
+    for copy in last_copies():
+        copy.start()
     for copy in e_copies(1)[EARLY:]:
         copy.start()
-    send_ens(2, n_var)
+    send_ens(2, last)
     with jax.named_scope("noise_x"):
         take_half(0)
+
+    with jax.named_scope("small"):
+        for k, has in ((0, r > 0), (1, r < regions - 1)):
+
+            @pl.when(has)
+            def _():
+                small_copy(k, after).wait_recv()
+
+            @pl.when(jnp.logical_not(has))
+            def _():
+                small[2 * k] = jnp.ones_like(small[1])
+                at = pl.ds(2 * k * n_obs, n_obs)
+                anom_t[at, :] = jnp.zeros((n_obs, MEMBERS), BF16)
+                gain[0, at, :] = jnp.zeros((n_obs, share), BF16)
+                pert[:, at] = jnp.zeros((MEMBERS, n_obs), BF16)
+
+    lane = lax.broadcasted_iota(jnp.int32, (n_obs, 128), 1)
+    shifts = (
+        jnp.where(r == 0, -16.0 * RADIUS, -RADIUS),
+        jnp.float32(0.0),
+        jnp.where(r == regions - 1, 16.0 * RADIUS, RADIUS),
+    )
+    with jax.named_scope("taper"):
+        for w in range(3):
+            spot = jnp.broadcast_to(small[w, 0:1, :] + shifts[w], (128, n_obs)).T
+            for k, quarter in enumerate((j, left)):
+                for c in range(share // 128):
+                    tile = (lane + (quarter * share + c * 128)).astype(F32)
+                    level = jnp.maximum(0.0, 1.0 - jnp.abs(tile - spot) / RADIUS)
+                    taper[k, pl.ds(w * n_obs, n_obs), pl.ds(c * 128, 128)] = level * level / (MEMBERS - 1)
 
     with jax.named_scope("sums"):
         three_sums = sums.at[pl.ds(0, 3)]
@@ -376,16 +392,21 @@
 
     def anomalies_of(l, slot):
         with jax.named_scope("take"):
-            block = recv.at[l, pl.ds(0, 3 * own), :]
-            remote(block, block, e_send, e_recv.at[l], member=opp).wait_recv()
+            for count, here in ((3, l < last), (2, l >= last)):
+
+                @pl.when(here)
+                def _():
+                    block = recv.at[l, pl.ds(0, count * own), :]
+                    remote(block, block, e_send, e_recv.at[l], member=opp).wait_recv()
+
         state = recv[l].astype(F32)
         mean = jnp.sum(state, axis=0, keepdims=True) / MEMBERS
         means[slot, 0:1, :] = mean
         anoms[slot] = (state - mean).astype(BF16)
 
-    def gain_of(slot, w):
+    def gain_of(slot, w, quarter=0):
         at = window(w)
-        gain[slot, at, :] = (dot(anom_t[at, :], anoms[slot]) * taper[at, :]).astype(BF16)
+        gain[slot, at, :] = (dot(anom_t[at, :], anoms[slot]) * taper[quarter, at, :]).astype(BF16)
 
     def perturbed(w, infl, root):
         mean, spread = tot[w, 0:1, :], tot[w, 1:2, :]
@@ -396,8 +417,9 @@
         pert[:, window(w)] = (moved * factor).astype(BF16)
 
     with jax.named_scope("anom0"):
-        pltpu.make_async_copy(ens_hbm.at[:, :, cols(j)], recv.at[:, rows(j), :], own_sem).wait()
         anomalies_of(0, 0)
+    with jax.named_scope("pass"):
+        pass_on()
     with jax.named_scope("pred_y"):
         from_depth(1)
     with jax.named_scope("gain0"):
@@ -451,28 +473,40 @@
         with jax.named_scope("inc"):
             increment = dot(pert[...], gain[slot])
             back[l] = (means[slot, 0:1, :] + root * anoms[slot].astype(F32) + increment).astype(BF16)
-        for copy in b_copies(l):
-            copy.start()
-        out[l, :, cols(j)] = back[l, rows(j), :]
-
-        @pl.when(l < n_var - 1)
+
+        @pl.when(l < last)
+        def _():
+            for copy in b_copies(l):
+                copy.start()
+            out[l, :, cols(j)] = back[l, rows(j), :]
+
+        for k, quarter, p in ((last, j, left), (last + 1, left, right)):
+
+            @pl.when(l == k)
+            def _():
+                remote(
+                    back.at[k, rows(p), :], out.at[last, :, cols(quarter)], b_send, b_recv, member=p
+                ).start()
+                out[last, :, cols(quarter)] = back[k, rows(j), :]
+
+        @pl.when(l <= last)
         def _():
             with jax.named_scope("gain"):
                 anomalies_of(l + 1, 1 - slot)
                 for w in range(3):
-                    gain_of(1 - slot, w)
+                    gain_of(1 - slot, w, (l + 1) // n_var)
 
         return c
 
-    lax.fori_loop(0, n_var, analyse, 0)
+    lax.fori_loop(0, n_var + 1, analyse, 0)
 
     with jax.named_scope("fin"):
-        back_in = back.at[:, pl.ds(0, 3 * own), :]
+        back_in = back.at[pl.ds(0, 5)]
         remote(back_in, back_in, b_send, b_recv, member=opp).wait_recv()
 
     with jax.named_scope("sent"):
         remote(back_in, back_in, b_send, b_recv, member=opp).wait_send()
-        ens_in = recv.at[:, pl.ds(0, 3 * own), :]
+        ens_in = recv.at[pl.ds(0, 6)]
         remote(ens_in, ens_in, e_send, e_recv.at[0], member=opp).wait_send()
         halves = obs.at[1, 0, pl.ds(0, 3 * own), :]
         remote(halves, halves, o_send, o_recv.at[0], member=opp).wait_send()
@@ -504,24 +538,22 @@
             pltpu.VMEM((1, n_obs), jnp.int32),
             pltpu.VMEM((3, 8, n_obs), F32),
             pltpu.VMEM((own, n_obs), F32),
-            pltpu.VMEM((own, n_tile), BF16),
-            pltpu.VMEM((n_tile, n_obs), BF16),
             pltpu.VMEM((2, own, n_obs), BF16),
             pltpu.VMEM((3, 2, members, n_obs), BF16),
             pltpu.VMEM((peers, 2, n_obs), F32),
             pltpu.VMEM((2, RING, 8, 128), F32),
-            pltpu.VMEM((n_var, members, share), BF16),
-            pltpu.VMEM((n_var, members, share), BF16),
+            pltpu.VMEM((n_var + 1, members, share), BF16),
+            pltpu.VMEM((n_var + 1, members, share), BF16),
             pltpu.VMEM((2, members, share), BF16),
             pltpu.VMEM((2, 8, share), F32),
             pltpu.VMEM((3 * n_obs, members), BF16),
-            pltpu.VMEM((3 * n_obs, share), F32),
+            pltpu.VMEM((2, 3 * n_obs, share), F32),
             pltpu.VMEM((2, 3 * n_obs, share), BF16),
             pltpu.VMEM((members, 3 * n_obs), BF16),
             pltpu.VMEM((3, 8, n_obs), F32),
             DMA((6,)),
             DMA,
-            DMA((n_var,)),
+            DMA((n_var + 3,)),
             DMA,
             DMA,
             DMA,
@@ -538,7 +570,6 @@
             DMA,
             DMA((2,)),
             DMA((2,)),
-            DMA,
         ]
         hbm = pl.BlockSpec(memory_space=pltpu.HBM)
         analysis, inflation = pl.pallas_call(

time: 46.6 us -> 45.9 us (0.985)
  no operation moved by 1% of the time
where the time goes in v6:
time: 45.9 us; the launch traced here: 45.8 us
  Pallas kernels  42.9 us (93%)
  between operations  1.8 us (4%)
  local copies, waits for them, and re-layouts  1.08 us (2%)
    pallas_call x1, Pallas kernels, shards(): pl.pallas_call(lambda *refs: kernel(regions, peers, RING, *refs), out_sha...  42.9 us
    unnamed x1, local copies, waits for them, and re-layouts  1.08 us

profile of v6, /device:TPU:1, one launch (start us, length us, event | category | flops | bytes accessed | tf_op | source)
XLA Modules:
  0.0 45.8 jit_solution(1544196401219118599)
XLA Ops:
  0.6 42.9 %shard_map.77 = (bf16[7,96,1024]{2,1,0:T(8,128)(2,1)S(1)}, f32[1,1]{1,0:T(1,128)S(1)}) custom-call(bf16[7,96,1024]{2,1,0:T(8,128)(2,1)} %refs_0_.1, f32[7]{0:T(128)} %refs_1_.1, s32[1,512]{1,0:T(1,128)} %bitcast.4, f32[1,512]{1,0:T(1,128)} %bitcast.5, f32[1,512]{1,0:T(1,128)} %bitcast.6, f32[96,512]{1,0:T(8,128)} %refs_5_.1), custom_call_target="tpu_custom_call" | custom-call | tf_op jit(solution)/shard_map/pallas_call | solution.py:575
  43.6 1.1 %copy.10 = bf16[7,96,1024]{2,1,0:T(8,128)(2,1)} copy(bf16[7,96,1024]{2,1,0:T(8,128)(2,1)S(1)} %get-tuple-element.6) | data formatting | bytes 2752512

commit v7 on v6

--- a/solution.py
+++ b/solution.py
@@ -9,7 +9,8 @@
 RADIUS = 1024.0
 RING = 4
 CHUNK = 256
-EARLY = 1
+TWICE = 2
+EARLY = 3
 MESH = pl.DeviceIdType.MESH
 F32 = jnp.float32
 BF16 = jnp.bfloat16
@@ -124,23 +125,25 @@
     for k, p, has, seam in sides:
         greeted = greeted + has.astype(jnp.int32) + seam.astype(jnp.int32)
 
+    rest = pl.ds(1, n_var - 1)
     loads = [
-        pltpu.make_async_copy(ens_hbm, ens, load_sem.at[0]),
-        pltpu.make_async_copy(wts_hbm, wts, load_sem.at[1]),
-        pltpu.make_async_copy(tiles_hbm, spots, load_sem.at[2]),
-        pltpu.make_async_copy(err_hbm, small.at[1, pl.ds(2, 1)], load_sem.at[3]),
-        pltpu.make_async_copy(vals_hbm, small.at[1, pl.ds(1, 1)], load_sem.at[4]),
-        pltpu.make_async_copy(noise_hbm, noise, load_sem.at[5]),
+        pltpu.make_async_copy(err_hbm, small.at[1, pl.ds(2, 1)], load_sem.at[0]),
+        pltpu.make_async_copy(noise_hbm, noise, load_sem.at[1]),
+        pltpu.make_async_copy(ens_hbm.at[0], ens.at[0], load_sem.at[2]),
+        pltpu.make_async_copy(tiles_hbm, spots, load_sem.at[3]),
+        pltpu.make_async_copy(wts_hbm, wts, load_sem.at[4]),
+        pltpu.make_async_copy(ens_hbm.at[rest], ens.at[rest], load_sem.at[5]),
+        pltpu.make_async_copy(vals_hbm, small.at[1, pl.ds(1, 1)], load_sem.at[6]),
     ]
     for copy in loads:
         copy.start()
 
     with jax.named_scope("noise"):
-        for copy in loads[3:]:
-            copy.wait()
+        loads[0].wait()
+        loads[1].wait()
         obs[1, 0, rows(j), :] = (jnp.sqrt(small[1, 2:3, :]) * noise[...]).astype(BF16)
     with jax.named_scope("ens"):
-        loads[0].wait()
+        loads[2].wait()
     with jax.named_scope("barrier"):
         pl.semaphore_wait(barrier, greeted)
 
@@ -158,25 +161,25 @@
 
         lax.fori_loop(first, last, body, 0)
 
-    last = n_var - 1
-
-    def last_copies():
-        to_right, to_left = dict(member=right), dict(member=left)
+    first = n_var - TWICE
+
+    def twice_copies(l):
+        far, rec = l + TWICE, n_var + TWICE + 2 * (l - first)
         return [
-            remote(ens.at[last, :, cols(right)], recv.at[last, rows(j), :], e_send, e_recv.at[last + 2], **to_right),
-            remote(ens.at[last, :, cols(opp)], recv.at[last + 1, rows(j), :], e_send, e_recv.at[last + 3], **to_left),
-            remote(ens.at[last, :, cols(j)], recv.at[last + 1, rows(j), :], e_send, e_recv.at[last + 1], **to_right),
-            remote(ens.at[last, :, cols(left)], recv.at[last, rows(j), :], e_send, e_recv.at[last], **to_left),
+            remote(ens.at[l, :, cols(right)], recv.at[l, rows(j), :], e_send, e_recv.at[rec], member=right),
+            remote(ens.at[l, :, cols(opp)], recv.at[far, rows(j), :], e_send, e_recv.at[rec + 1], member=left),
+            remote(ens.at[l, :, cols(j)], recv.at[far, rows(j), :], e_send, e_recv.at[far], member=right),
+            remote(ens.at[l, :, cols(left)], recv.at[l, rows(j), :], e_send, e_recv.at[l], member=left),
         ]
 
-    def pass_on():
-        first, second, _, _ = last_copies()
-        block = recv.at[last, rows(left), :]
-        first.wait_recv()
-        remote(block, recv.at[last + 1, rows(left), :], e_send, e_recv.at[last + 1], member=right).start()
-        block = recv.at[last + 1, rows(right), :]
-        second.wait_recv()
-        remote(block, recv.at[last, rows(right), :], e_send, e_recv.at[last], member=left).start()
+    def pass_on(l):
+        far, copies = l + TWICE, twice_copies(l)
+        block = recv.at[l, rows(left), :]
+        copies[0].wait_recv()
+        remote(block, recv.at[far, rows(left), :], e_send, e_recv.at[far], member=right).start()
+        block = recv.at[far, rows(right), :]
+        copies[1].wait_recv()
+        remote(block, recv.at[l, rows(right), :], e_send, e_recv.at[l], member=left).start()
 
     def o_copies(q):
         block = obs.at[1, q, rows(j), half(d)]
@@ -245,12 +248,11 @@
     for copy in o_copies(0):
         copy.start()
     send_ens(0, 1)
+    with jax.named_scope("load_all"):
+        for copy in loads[3:]:
+            copy.wait()
     for copy in e_copies(1)[:EARLY]:
         copy.start()
-
-    with jax.named_scope("load_small"):
-        loads[1].wait()
-        loads[2].wait()
     with jax.named_scope("pick"):
         spot_row = spots[...]
         picked = None
@@ -279,7 +281,8 @@
         return c
 
     lax.fori_loop(0, n_var, take_own, 0)
-    recv[last + 1, rows(j), :] = ens[last, :, cols(left)]
+    for l in range(first, n_var):
+        recv[l + TWICE, rows(j), :] = ens[l, :, cols(left)]
 
     with jax.named_scope("swap"):
         swap.wait_recv()
@@ -296,11 +299,12 @@
     for copy in m_copies + o_copies(1):
         copy.start()
     to_beside(1, j)
-    for copy in last_copies():
-        copy.start()
+    for l in range(first, n_var):
+        for copy in twice_copies(l):
+            copy.start()
     for copy in e_copies(1)[EARLY:]:
         copy.start()
-    send_ens(2, last)
+    send_ens(2, first)
     with jax.named_scope("noise_x"):
         take_half(0)
 
@@ -392,7 +396,7 @@
 
     def anomalies_of(l, slot):
         with jax.named_scope("take"):
-            for count, here in ((3, l < last), (2, l >= last)):
+            for count, here in ((3, l < first), (2, l >= first)):
 
                 @pl.when(here)
                 def _():
@@ -419,7 +423,8 @@
     with jax.named_scope("anom0"):
         anomalies_of(0, 0)
     with jax.named_scope("pass"):
-        pass_on()
+        for l in range(first, n_var):
+            pass_on(l)
     with jax.named_scope("pred_y"):
         from_depth(1)
     with jax.named_scope("gain0"):
@@ -474,22 +479,23 @@
             increment = dot(pert[...], gain[slot])
             back[l] = (means[slot, 0:1, :] + root * anoms[slot].astype(F32) + increment).astype(BF16)
 
-        @pl.when(l < last)
+        @pl.when(l < first)
         def _():
             for copy in b_copies(l):
                 copy.start()
             out[l, :, cols(j)] = back[l, rows(j), :]
 
-        for k, quarter, p in ((last, j, left), (last + 1, left, right)):
-
-            @pl.when(l == k)
+        for here, at, quarter, p in (
+            (jnp.logical_and(l >= first, l < n_var), l, j, left),
+            (l >= n_var, l - TWICE, left, right),
+        ):
+
+            @pl.when(here)
             def _():
-                remote(
-                    back.at[k, rows(p), :], out.at[last, :, cols(quarter)], b_send, b_recv, member=p
-                ).start()
-                out[last, :, cols(quarter)] = back[k, rows(j), :]
-
-        @pl.when(l <= last)
+                remote(back.at[l, rows(p), :], out.at[at, :, cols(quarter)], b_send, b_recv, member=p).start()
+                out[at, :, cols(quarter)] = back[l, rows(j), :]
+
+        @pl.when(l < n_var + TWICE - 1)
         def _():
             with jax.named_scope("gain"):
                 anomalies_of(l + 1, 1 - slot)
@@ -498,15 +504,17 @@
 
         return c
 
-    lax.fori_loop(0, n_var + 1, analyse, 0)
+    lax.fori_loop(0, n_var + TWICE, analyse, 0)
 
     with jax.named_scope("fin"):
-        back_in = back.at[pl.ds(0, 5)]
+        got = (3 * n_var - TWICE) * own
+        deep = next(k for k in range(1, n_var) if got % (16 * k) == 0 and got // k <= peers * own)
+        back_in = back.at[pl.ds(0, deep), pl.ds(0, got // deep), :]
         remote(back_in, back_in, b_send, b_recv, member=opp).wait_recv()
 
     with jax.named_scope("sent"):
         remote(back_in, back_in, b_send, b_recv, member=opp).wait_send()
-        ens_in = recv.at[pl.ds(0, 6)]
+        ens_in = recv.at[:, pl.ds(0, 3 * own), :]
         remote(ens_in, ens_in, e_send, e_recv.at[0], member=opp).wait_send()
         halves = obs.at[1, 0, pl.ds(0, 3 * own), :]
         remote(halves, halves, o_send, o_recv.at[0], member=opp).wait_send()
@@ -542,8 +550,8 @@
             pltpu.VMEM((3, 2, members, n_obs), BF16),
             pltpu.VMEM((peers, 2, n_obs), F32),
             pltpu.VMEM((2, RING, 8, 128), F32),
-            pltpu.VMEM((n_var + 1, members, share), BF16),
-            pltpu.VMEM((n_var + 1, members, share), BF16),
+            pltpu.VMEM((n_var + TWICE, members, share), BF16),
+            pltpu.VMEM((n_var + TWICE, members, share), BF16),
             pltpu.VMEM((2, members, share), BF16),
             pltpu.VMEM((2, 8, share), F32),
             pltpu.VMEM((3 * n_obs, members), BF16),
@@ -551,9 +559,9 @@
             pltpu.VMEM((2, 3 * n_obs, share), BF16),
             pltpu.VMEM((members, 3 * n_obs), BF16),
             pltpu.VMEM((3, 8, n_obs), F32),
-            DMA((6,)),
-            DMA,
-            DMA((n_var + 3,)),
+            DMA((7,)),
+            DMA,
+            DMA((n_var + 3 * TWICE,)),
             DMA,
             DMA,
             DMA,

time: 45.9 us -> 45.7 us (level)
  no operation moved by 1% of the time
where the time goes in v7:
time: 45.7 us; the launch traced here: 45.5 us
  Pallas kernels  42.6 us (93%)
  between operations  1.8 us (4%)
  local copies, waits for them, and re-layouts  1.08 us (2%)
    pallas_call x1, Pallas kernels, shards(): pl.pallas_call(lambda *refs: kernel(regions, peers, RING, *refs), out_sha...  42.6 us
    unnamed x1, local copies, waits for them, and re-layouts  1.08 us

profile of v7, /device:TPU:1, one launch (start us, length us, event | category | flops | bytes accessed | tf_op | source)
XLA Modules:
  0.0 45.5 jit_solution(14752711407543971416)
XLA Ops:
  0.6 42.6 %shard_map.77 = (bf16[7,96,1024]{2,1,0:T(8,128)(2,1)S(1)}, f32[1,1]{1,0:T(1,128)S(1)}) custom-call(bf16[7,96,1024]{2,1,0:T(8,128)(2,1)} %refs_0_.1, f32[7]{0:T(128)} %refs_1_.1, s32[1,512]{1,0:T(1,128)} %bitcast.4, f32[1,512]{1,0:T(1,128)} %bitcast.5, f32[1,512]{1,0:T(1,128)} %bitcast.6, f32[96,512]{1,0:T(8,128)} %refs_5_.1), custom_call_target="tpu_custom_call" | custom-call | tf_op jit(solution)/shard_map/pallas_call | solution.py:583
  43.3 1.1 %copy.10 = bf16[7,96,1024]{2,1,0:T(8,128)(2,1)} copy(bf16[7,96,1024]{2,1,0:T(8,128)(2,1)S(1)} %get-tuple-element.6) | data formatting | bytes 2752512

commit v8 on v7

--- a/solution.py
+++ b/solution.py
@@ -10,7 +10,7 @@
 RING = 4
 CHUNK = 256
 TWICE = 2
-EARLY = 3
+EARLY = (3, 1)
 MESH = pl.DeviceIdType.MESH
 F32 = jnp.float32
 BF16 = jnp.bfloat16
@@ -251,8 +251,13 @@
     with jax.named_scope("load_all"):
         for copy in loads[3:]:
             copy.wait()
-    for copy in e_copies(1)[:EARLY]:
-        copy.start()
+    for h, count in enumerate(EARLY):
+
+        @pl.when(d == h)
+        def _():
+            for copy in e_copies(1)[:count]:
+                copy.start()
+
     with jax.named_scope("pick"):
         spot_row = spots[...]
         picked = None
@@ -302,8 +307,13 @@
     for l in range(first, n_var):
         for copy in twice_copies(l):
             copy.start()
-    for copy in e_copies(1)[EARLY:]:
-        copy.start()
+    for h, count in enumerate(EARLY):
+
+        @pl.when(d == h)
+        def _():
+            for copy in e_copies(1)[count:]:
+                copy.start()
+
     send_ens(2, first)
     with jax.named_scope("noise_x"):
         take_half(0)
@@ -422,11 +432,11 @@
 
     with jax.named_scope("anom0"):
         anomalies_of(0, 0)
+    with jax.named_scope("pred_y"):
+        from_depth(1)
     with jax.named_scope("pass"):
         for l in range(first, n_var):
             pass_on(l)
-    with jax.named_scope("pred_y"):
-        from_depth(1)
     with jax.named_scope("gain0"):
         turned(1, tot[1, 0:1, :])
         gain_of(0, 1)

time: 45.7 us -> 45.1 us (0.987)
  Pallas kernels: 42.6 us -> 42.1 us
    pallas_call x1, Pallas kernels: 42.6 us -> 42.1 us  [shards(): pl.pallas_call(lambda *refs: kernel(regions, peers, RING, *refs), out_sha...]
where the time goes in v8:
time: 45.1 us; the launch traced here: 45 us
  Pallas kernels  42.1 us (93%)
  between operations  1.8 us (4%)
  local copies, waits for them, and re-layouts  1.08 us (2%)
    pallas_call x1, Pallas kernels, shards(): pl.pallas_call(lambda *refs: kernel(regions, peers, RING, *refs), out_sha...  42.1 us
    unnamed x1, local copies, waits for them, and re-layouts  1.08 us

profile of v8, /device:TPU:1, one launch (start us, length us, event | category | flops | bytes accessed | tf_op | source)
XLA Modules:
  0.0 45.0 jit_solution(3233822785356825040)
XLA Ops:
  0.6 42.1 %shard_map.77 = (bf16[7,96,1024]{2,1,0:T(8,128)(2,1)S(1)}, f32[1,1]{1,0:T(1,128)S(1)}) custom-call(bf16[7,96,1024]{2,1,0:T(8,128)(2,1)} %refs_0_.1, f32[7]{0:T(128)} %refs_1_.1, s32[1,512]{1,0:T(1,128)} %bitcast.4, f32[1,512]{1,0:T(1,128)} %bitcast.5, f32[1,512]{1,0:T(1,128)} %bitcast.6, f32[96,512]{1,0:T(8,128)} %refs_5_.1), custom_call_target="tpu_custom_call" | custom-call | tf_op jit(solution)/shard_map/pallas_call | solution.py:593
  42.7 1.1 %copy.10 = bf16[7,96,1024]{2,1,0:T(8,128)(2,1)} copy(bf16[7,96,1024]{2,1,0:T(8,128)(2,1)S(1)} %get-tuple-element.6) | data formatting | bytes 2752512

commit v9 on v8

--- a/solution.py
+++ b/solution.py
@@ -440,11 +440,14 @@
     with jax.named_scope("gain0"):
         turned(1, tot[1, 0:1, :])
         gain_of(0, 1)
-    with jax.named_scope("near1"):
-        beside(1, near).wait_recv()
-    with jax.named_scope("gainn"):
-        stats(near)
-        gain_of(0, near)
+    def near_gain():
+        with jax.named_scope("near1"):
+            beside(1, near).wait_recv()
+        with jax.named_scope("gainn"):
+            stats(near)
+            gain_of(0, near)
+
+    pl.when(core == 0)(near_gain)
 
     def far_gain():
         with jax.named_scope("far1"):
@@ -463,6 +466,7 @@
     infl_ref[...] = infl
     with jax.named_scope("pert1"):
         perturbed(1, infl, root)
+    pl.when(core == 1)(near_gain)
     with jax.named_scope("near0"):
         beside(0, near).wait_recv()
     with jax.named_scope("pertn"):

time: 45.1 us -> 45.1 us (level)
  no operation moved by 1% of the time
where the time goes in v9:
time: 45.1 us; the launch traced here: 45 us
  Pallas kernels  42.1 us (93%)
  between operations  1.8 us (4%)
  local copies, waits for them, and re-layouts  1.08 us (2%)
    pallas_call x1, Pallas kernels, shards(): pl.pallas_call(lambda *refs: kernel(regions, peers, RING, *refs), out_sha...  42.1 us
    unnamed x1, local copies, waits for them, and re-layouts  1.08 us

profile of v9, /device:TPU:1, one launch (start us, length us, event | category | flops | bytes accessed | tf_op | source)
XLA Modules:
  0.0 45.0 jit_solution(621628493488761264)
XLA Ops:
  0.6 42.1 %shard_map.77 = (bf16[7,96,1024]{2,1,0:T(8,128)(2,1)S(1)}, f32[1,1]{1,0:T(1,128)S(1)}) custom-call(bf16[7,96,1024]{2,1,0:T(8,128)(2,1)} %refs_0_.1, f32[7]{0:T(128)} %refs_1_.1, s32[1,512]{1,0:T(1,128)} %bitcast.4, f32[1,512]{1,0:T(1,128)} %bitcast.5, f32[1,512]{1,0:T(1,128)} %bitcast.6, f32[96,512]{1,0:T(8,128)} %refs_5_.1), custom_call_target="tpu_custom_call" | custom-call | tf_op jit(solution)/shard_map/pallas_call | solution.py:597
  42.7 1.1 %copy.10 = bf16[7,96,1024]{2,1,0:T(8,128)(2,1)} copy(bf16[7,96,1024]{2,1,0:T(8,128)(2,1)S(1)} %get-tuple-element.6) | data formatting | bytes 2752512
